TPU v7x, 32 devices: a whole 2x2x4 slice. The times are simulated.
32 devices in a mesh: vol: 8 (over z, y), pix: 4 (over x, core).
Axes of the slice: x: 2, y: 2, z: 4, core: 2. Of those that a mesh axis runs over, the one named last changes fastest.
Arguments:
- kernel: bfloat16 [524288, 128], P(('vol', 'pix')), may hold values from 0 to 0.25
- pressure: bfloat16 [524288], P(('vol', 'pix')), may hold values from 0.049804688 to 2
- velocity: bfloat16 [524288], P(('vol', 'pix')), may hold values from -4 to 4
- entry_slot: int32 [32, 16384], P(('vol', 'pix')), may hold values from 0 to 1023, never falling along the last dimension, each value on 1 to 32 neighbouring positions
- slot_tile: int32 [32, 1024], P(('vol', 'pix')), may hold values from 0 to 8191, as said below
- tile_owner: int32 [8192], replicated, may hold values from 0 to 3, as said below
Outputs:
- owned_tiles: float32 [16384, 256], P(('vol', 'pix'))
- shell_map: float32 [8192, 256], P('vol')
Inputs may be any that keep to these rules, and one draw needn't show every extreme that they name: `entry_slot`: for each device the slot numbers never fall along its 16384 crossings; every slot has at least one crossing and at most 32. `tile_owner`: within every block of 1024 consecutive tiles each pix index owns 256 // 2 to 512 tiles, and one owner of each block owns exactly 512. `slot_tile`: the 1024 tiles of one device are distinct; at most 64 of them belong to any one owning device (vol index t // 1024, pix index tile_owner[t]), and one owning device gets exactly 64 from every device.
All inputs are finite; a program needn't handle non-finite values.
Results may differ from a plain program's by a relative error of at most 0.0003.
Values sent between devices are 32-bit elements; how exact they have to be, the bound alone decides.
A program may use at most 64 MiB of HBM per device.

v0:
```python
import functools

import jax
import jax.numpy as jnp
from jax import lax
from jax.experimental import pallas as pl
from jax.experimental.pallas import tpu as pltpu
from jax.sharding import PartitionSpec as P

MESH = pl.DeviceIdType.MESH
LANES = 128
BLOCK = 256
WINDOW = 48
F32 = jnp.float32
BF16 = jnp.bfloat16
I32 = jnp.int32


def iota(shape, axis):
    return lax.broadcasted_iota(I32, shape, axis)


def onehot(mask):
    return jnp.where(mask, 1.0, 0.0).astype(BF16)


def dot(a, b):
    return jnp.dot(a, b, preferred_element_type=F32)


def halves(x):
    high = x.astype(BF16)
    low = (x - high.astype(F32)).astype(BF16)
    return jnp.concatenate([high, low], axis=1)


def prepare(
    dims, base_ref, last_ref, kern_hbm, thermal_ref, kinetic_ref, slot_ref, tile_ref, owner_ref,
    out_ref, ids_ref, code_ref, kern_ref, thermal32, kinetic32, part_ref, split_ref, all_codes,
    sems,
):
    vol_count, pix_count, slots, block_tiles, owned_most, cap = dims
    device_count = vol_count * pix_count
    entries = kern_ref.shape[0]
    blocks = entries // BLOCK
    pieces = sems.shape[0]
    piece = entries // pieces

    def fetch(q):
        rows = pl.ds(q * piece, piece)
        return pltpu.make_async_copy(kern_hbm.at[rows], kern_ref.at[rows], sems.at[q])

    for q in range(pieces):
        fetch(q).start()

    high_count = owner_ref.shape[0]
    block_high = block_tiles // LANES
    owner = jnp.transpose(owner_ref[...].astype(F32))
    lower = onehot(iota((LANES, LANES), 1) < iota((LANES, LANES), 0))
    first, second = iota((high_count, high_count), 0), iota((high_count, high_count), 1)
    before = onehot((first < second) & (first // block_high == second // block_high))
    rank = jnp.zeros((LANES, high_count), F32)
    for p in range(pix_count):
        mine = owner == p
        ones = jnp.where(mine, 1.0, 0.0)
        inside = dot(lower, ones.astype(BF16))
        total = jnp.broadcast_to(jnp.sum(ones, axis=0, keepdims=True), (8, high_count))
        ahead = dot(total.astype(BF16), before)[0:1]
        rank = rank + jnp.where(mine, inside + ahead, 0.0)

    all_codes[...] = jnp.transpose(owner * owned_most + rank).astype(I32)
    first_high = pl.multiple_of(lax.axis_index("vol") * block_high, block_high)
    code_ref[...] = all_codes[pl.ds(first_high, block_high), :]

    parts = max(1, owned_most // 256)
    rank_high = jnp.floor(rank * (1.0 / 256.0))
    rank_low = rank - 256.0 * rank_high
    table = jnp.concatenate([owner * parts + rank_high, rank_low], axis=0).astype(BF16)
    tile = tile_ref[...]
    high, low = tile // LANES, tile % LANES
    found = dot(table, onehot(iota((high_count, slots), 0) == high))
    pick = iota((LANES, slots), 0) == low
    both = jnp.sum(jnp.where(pick, found[:LANES], 0.0), axis=0, keepdims=True).astype(I32)
    row_low = jnp.sum(jnp.where(pick, found[LANES:], 0.0), axis=0, keepdims=True)
    slot_owner = both // parts
    row_high = (both - slot_owner * parts).astype(F32)
    target = high // block_high * pix_count + slot_owner
    to_device = iota((device_count, slots), 0) == target
    ones = jnp.where(to_device, 1.0, 0.0)
    upper = onehot(iota((LANES, LANES), 0) < iota((LANES, LANES), 1))
    carry = jnp.zeros((device_count, 1), F32)
    position = []
    for j in range(slots // LANES):
        chunk = ones[:, j * LANES:(j + 1) * LANES]
        ranks = dot(chunk.astype(BF16), upper) + carry
        position.append(jnp.sum(chunk * ranks, axis=0, keepdims=True))
        carry = carry + jnp.sum(chunk, axis=1, keepdims=True)
    position = jnp.concatenate(position, axis=1).astype(I32)
    bucket = target * cap + position

    places = onehot(iota((LANES, slots), 0) % cap == position)
    values = jnp.concatenate(
        [jnp.where(to_device, row_high, 0.0), jnp.where(to_device, row_low + 1.0, 0.0)], axis=0
    )
    placed = lax.dot_general(
        values.astype(BF16), places, (((1,), (1,)), ((), ())), preferred_element_type=F32
    )
    rows = placed[:device_count] * 256.0 + placed[device_count:] - 1.0
    ids_ref[...] = jnp.broadcast_to(
        rows.astype(I32)[:, None, :], (device_count, 8, LANES)
    )

    thermal32[...] = thermal_ref[...].astype(F32)
    kinetic32[...] = kinetic_ref[...].astype(F32)
    part_ref[...] = jnp.zeros_like(part_ref)
    within = iota((WINDOW, BLOCK), 0)

    def add_window(i, base):
        def pair(ref):
            return jnp.concatenate([ref[pl.ds(2 * i, 1), :], ref[pl.ds(2 * i + 1, 1), :]], axis=1)

        base = pl.multiple_of(base, 8)
        match = within + base == pair(slot_ref)
        weights = jnp.concatenate(
            [jnp.where(match, pair(thermal32), 0.0), jnp.where(match, pair(kinetic32), 0.0)], axis=0
        ).astype(BF16)
        sums = dot(weights, kern_ref[pl.ds(pl.multiple_of(i * BLOCK, BLOCK), BLOCK), :])
        part_ref[pl.ds(base, WINDOW), 0:LANES] += sums[:WINDOW]
        part_ref[pl.ds(base, WINDOW), LANES:2 * LANES] += sums[WINDOW:]

    per = blocks // pieces
    for q in range(pieces):
        fetch(q).wait()

        def first_window(i, unused):
            add_window(i, base_ref[i])
            return unused

        lax.fori_loop(q * per, (q + 1) * per, first_window, 0, unroll=4)

    def more_windows(i, unused):
        base = base_ref[i]
        extra = (last_ref[i] - base) // WINDOW

        def one(w, unused):
            add_window(i, base + w * WINDOW)
            return unused

        return lax.fori_loop(1, extra + 1, one, unused)

    lax.fori_loop(0, blocks, more_windows, 0)

    split_ref[...] = halves(part_ref[0:slots, :])
    some = min(256, device_count * cap)

    def permute(i, unused):
        start = pl.multiple_of(i * some, some)
        moved = dot(onehot(iota((some, slots), 0) + start == bucket), split_ref[...])
        out_ref[pl.ds(start, some), :] = moved[:, :2 * LANES] + moved[:, 2 * LANES:]
        return unused

    lax.fori_loop(0, device_count * cap // some, permute, 0)


def exchange(
    dims, out_hbm, ids_hbm, code_ref, owned_ref, shell_ref, arrived, ids, sums, crossed, gathered,
    send_sem, recv_sem, ids_send, ids_recv, local_sem, mid_send, mid_recv, own_send, own_recv,
    far_send, far_recv, pass_send, pass_recv,
):
    vol_count, pix_count, slots, block_tiles, owned_most, cap = dims
    half = vol_count // 2
    near_count = half * pix_count
    vol, pix = lax.axis_index("vol"), lax.axis_index("pix")
    side, place = vol // half, vol % half
    mine = place * pix_count + pix
    across = (vol + half) % vol_count
    width = 2 * LANES

    def peer(k):
        return side * half + (place + k // pix_count) % half, (pix + k % pix_count) % pix_count

    barrier = pltpu.get_barrier_semaphore()

    def greet(k, unused):
        pl.semaphore_signal(barrier, inc=1, device_id=peer(k), device_id_type=MESH)
        return unused

    pl.semaphore_signal(barrier, inc=1, device_id=(across, pix), device_id_type=MESH)
    lax.fori_loop(1, near_count, greet, 0)
    pl.semaphore_wait(barrier, near_count)

    def final(stage, other_vol, other_pix):
        return (other_vol + half * (1 - stage)) % vol_count * pix_count + other_pix

    def ids_copy(stage, k):
        other_vol, other_pix = peer(k)
        return pltpu.make_async_remote_copy(
            src_ref=ids_hbm.at[final(stage, other_vol, other_pix)], dst_ref=ids.at[stage, mine],
            send_sem=ids_send.at[stage, k], recv_sem=ids_recv.at[stage, k],
            device_id=(other_vol, other_pix), device_id_type=MESH,
        )

    def rows_copy(stage, k):
        other_vol, other_pix = peer(k)
        return pltpu.make_async_remote_copy(
            src_ref=out_hbm.at[pl.ds(final(stage, other_vol, other_pix) * cap, cap)],
            dst_ref=arrived.at[stage, pl.ds(mine * cap, cap)],
            send_sem=send_sem.at[stage, k], recv_sem=recv_sem.at[stage, k],
            device_id=(other_vol, other_pix), device_id_type=MESH,
        )

    def local_copies(stage):
        own = final(stage, vol, pix)
        return (
            pltpu.make_async_copy(ids_hbm.at[own], ids.at[stage, mine], local_sem.at[stage, 0]),
            pltpu.make_async_copy(
                out_hbm.at[pl.ds(own * cap, cap)], arrived.at[stage, pl.ds(mine * cap, cap)],
                local_sem.at[stage, 1],
            ),
        )

    for stage in range(2):

        def send(k, unused):
            ids_copy(stage, k).start()
            rows_copy(stage, k).start()
            return unused

        for copy in local_copies(stage):
            copy.start()
        lax.fori_loop(1, near_count, send, 0)

    group = pix_count * cap
    share = LANES // cap
    lane_part = iota((1, LANES), 1) // cap

    def sum_up(stage, target):
        for copy in local_copies(stage):
            copy.wait()
        target[...] = jnp.zeros((owned_most, width), F32)

        def receive(i, unused):
            def one(j, unused):
                k = i * pix_count + j
                ids_copy(stage, k).wait_recv()
                rows_copy(stage, k).wait_recv()
                return unused

            lax.fori_loop(jnp.where(i == 0, 1, 0), pix_count, one, 0)
            sender = (place + half - i) % half
            pieces = []
            for tau in range(group // LANES):
                piece = jnp.full((1, LANES), -1, I32)
                for g in range(share):
                    line = ids[stage, sender * pix_count + tau * share + g]
                    piece = jnp.where(lane_part == g, line[0:1], piece)
                pieces.append(piece)
            rows = jnp.concatenate(pieces, axis=1) if len(pieces) > 1 else pieces[0]
            places = onehot(iota((owned_most, group), 0) == rows)
            start = pl.multiple_of(sender * group, group)
            moved = dot(places, halves(arrived[stage, pl.ds(start, group), :]))
            target[...] += moved[:, :width] + moved[:, width:]
            return unused

        lax.fori_loop(0, half, receive, 0)

    piece_count = mid_send.shape[0]
    piece_rows = owned_most // piece_count

    def part(q):
        return pl.ds(q * piece_rows, piece_rows)

    def mid_copy(q):
        return pltpu.make_async_remote_copy(
            src_ref=sums.at[part(q)], dst_ref=crossed.at[part(q)],
            send_sem=mid_send.at[q], recv_sem=mid_recv.at[q],
            device_id=(across, pix), device_id_type=MESH,
        )

    sum_up(0, sums)
    for q in range(piece_count):
        mid_copy(q).start()
    own = gathered.at[pix]
    sum_up(1, own)

    core = pix % 2
    sibling = (vol, pix - core + (1 - core))
    others = range(1, pix_count // 2)

    def far_copy(k, q):
        return pltpu.make_async_remote_copy(
            src_ref=gathered.at[pix, part(q)], dst_ref=gathered.at[pix, part(q)],
            send_sem=far_send.at[k, q], recv_sem=far_recv.at[k, q],
            device_id=(vol, (pix + 2 * k) % pix_count), device_id_type=MESH,
        )

    def pass_copy(k, q):
        source = (pix + pix_count - 2 * k) % pix_count
        return pltpu.make_async_remote_copy(
            src_ref=gathered.at[source, part(q)], dst_ref=gathered.at[source, part(q)],
            send_sem=pass_send.at[k, q], recv_sem=pass_recv.at[k, q],
            device_id=sibling, device_id_type=MESH,
        )

    def own_copy(q):
        return pltpu.make_async_remote_copy(
            src_ref=gathered.at[pix, part(q)], dst_ref=gathered.at[pix, part(q)],
            send_sem=own_send.at[q], recv_sem=own_recv.at[q],
            device_id=sibling, device_id_type=MESH,
        )

    def relay(q):
        for k in others:
            far_copy(k, q).wait_recv()
            pass_copy(k, q).start()

    for q in range(piece_count):
        mid_copy(q).wait_recv()
        whole = own[part(q), :] + crossed[part(q), :]
        own[part(q), :] = whole
        owned_ref[part(q), :] = whole
        for k in others:
            far_copy(k, q).start()
        own_copy(q).start()
        if q:
            relay(q - 1)
    relay(piece_count - 1)
    for q in range(piece_count):
        own_copy(q).wait()
        mid_copy(q).wait_send()
        for k in others:
            far_copy(k, q).wait_send()
            pass_copy(k, q).wait()

    def gather(i, unused):
        lines = []
        for j in range(8):
            code = code_ref[i * 8 + j]
            source = code // owned_most
            lines.append(gathered[source, pl.ds(code - source * owned_most, 1), :])
        shell_ref[pl.ds(pl.multiple_of(i * 8, 8), 8), :] = jnp.concatenate(lines, axis=0)
        return unused

    lax.fori_loop(0, block_tiles // 8, gather, 0, unroll=2)

    for stage in range(2):

        def sent(k, unused):
            ids_copy(stage, k).wait_send()
            rows_copy(stage, k).wait_send()
            return unused

        lax.fori_loop(1, near_count, sent, 0)


def shards(kernel, pressure, velocity, entry_slot, slot_tile, tile_owner):
    vol_count, pix_count = lax.axis_size("vol"), lax.axis_size("pix")
    device_count = vol_count * pix_count
    entries = kernel.shape[0]
    slots = slot_tile.shape[1]
    tiles = tile_owner.shape[0]
    block_tiles = tiles // vol_count
    owned_most = 2 * block_tiles // pix_count
    cap = 2 * slots // device_count
    width = 2 * kernel.shape[1]
    dims = (vol_count, pix_count, slots, block_tiles, owned_most, cap)
    vmem = pl.BlockSpec(memory_space=pltpu.VMEM)
    smem = pl.BlockSpec(memory_space=pltpu.SMEM)
    anywhere = pl.BlockSpec(memory_space=pl.ANY)
    dma = pltpu.SemaphoreType.DMA

    ends = entry_slot.reshape(entries // BLOCK, BLOCK)
    base = ends[:, 0] // 8 * 8
    last = ends[:, BLOCK - 1]
    shape = (entries // LANES, LANES)
    outgoing, ids, codes = pl.pallas_call(
        functools.partial(prepare, dims),
        out_shape=(
            jax.ShapeDtypeStruct((device_count * cap, width), F32),
            jax.ShapeDtypeStruct((device_count, 8, LANES), I32),
            jax.ShapeDtypeStruct((block_tiles // LANES, LANES), I32),
        ),
        in_specs=[smem, smem, anywhere, vmem, vmem, vmem, vmem, vmem],
        out_specs=(vmem, vmem, vmem),
        scratch_shapes=[
            pltpu.VMEM(kernel.shape, BF16),
            pltpu.VMEM(shape, F32),
            pltpu.VMEM(shape, F32),
            pltpu.VMEM((slots + WINDOW, width), F32),
            pltpu.VMEM((slots, 2 * width), BF16),
            pltpu.VMEM((tiles // LANES, LANES), I32),
            dma((4,)),
        ],
        name="prepare",
    )(
        base, last, kernel, pressure.reshape(shape), velocity.reshape(shape),
        entry_slot.reshape(shape), slot_tile, tile_owner.reshape(tiles // LANES, LANES),
    )

    pieces = 4
    chips = pix_count // 2
    near = device_count // 2
    return pl.pallas_call(
        functools.partial(exchange, dims),
        out_shape=(
            jax.ShapeDtypeStruct((owned_most, width), F32),
            jax.ShapeDtypeStruct((block_tiles, width), F32),
        ),
        in_specs=[anywhere, anywhere, smem],
        out_specs=(vmem, vmem),
        scratch_shapes=[
            pltpu.VMEM((2, near * cap, width), F32),
            pltpu.VMEM((2, near, 8, LANES), I32),
            pltpu.VMEM((owned_most, width), F32),
            pltpu.VMEM((owned_most, width), F32),
            pltpu.VMEM((pix_count, owned_most, width), F32),
            dma((2, near)), dma((2, near)), dma((2, near)), dma((2, near)),
            dma((2, 2)), dma((pieces,)), dma((pieces,)), dma((pieces,)), dma((pieces,)),
            dma((chips, pieces)), dma((chips, pieces)), dma((chips, pieces)), dma((chips, pieces)),
        ],
        compiler_params=pltpu.CompilerParams(collective_id=0, has_side_effects=True),
        name="exchange",
    )(outgoing, ids, codes.reshape(block_tiles))


def solution(mesh):
    in_specs = (
        P(("vol", "pix"), None),
        P(("vol", "pix")),
        P(("vol", "pix")),
        P(("vol", "pix"), None),
        P(("vol", "pix"), None),
        P(),
    )
    out_specs = (P(("vol", "pix"), None), P("vol", None))
    return jax.shard_map(shards, mesh=mesh, in_specs=in_specs, out_specs=out_specs, check_vma=False)
```

profile of v0, /device:TPU:29, one launch (start us, length us, event | category | flops | bytes accessed | tf_op | source)
XLA Modules:
  0.0 87.2 jit_solution(1033021302380785238)
XLA Ops:
  0.6 0.5 broadcast.12
  1.1 1.6 %reduce.3 = s32[16384]{0:T(1024)S(1)} reduce(s32[1,16384]{1,0:T(1,128)} %param.9, s32[]{:T(128)} %broadcast.12), dimensions={0}, to_apply=%param.9.reduce_sub_computation.3 | reduce | bytes 131076 | tf_op args[3]
  2.8 0.1 fusion.1
  2.9 0.6 copy.11
  3.5 0.1 copy.10
  3.6 0.6 fusion.base_ref
  4.1 12.2 %prepare.1 = (f32[2048,256]{1,0:T(8,128)}, s32[32,8,128]{2,1,0:T(8,128)}, s32[8,128]{1,0:T(8,128)}) custom-call(s32[64]{0:T(128)} %fusion.base_ref, s32[64]{0:T(128)} %bitcast.21, bf16[16384,128]{1,0:T(8,128)(2,1)} %kern_hbm.1, bf16[128,128]{1,0:T(8,128)(2,1)} %bitcast.17, bf16[128,128]{1,0:T(8,128)(2,1)} %bitcast.18, s32[128,128]{1,0:T(8,128)} %bitcast.16, ...), custom_call_target="tpu_custom_call" | custom-call | tf_op jit(solution)/shard_map/prepare/pallas_call | solution.py:376
  16.3 66.8 %exchange.1 = (f32[512,256]{1,0:T(8,128)}, f32[1024,256]{1,0:T(8,128)}) custom-call(f32[2048,256]{1,0:T(8,128)} %get-tuple-element.5.out_hbm, s32[32,8,128]{2,1,0:T(8,128)} %get-tuple-element.6.ids_hbm, s32[1024]{0:T(1024)} %bitcast.20), custom_call_target="tpu_custom_call" | custom-call | tf_op jit(solution)/shard_map/exchange/pallas_call | solution.py:403
  83.1 1.9 %copy.14 = f32[512,256]{1,0:T(8,128)} copy(f32[512,256]{1,0:T(8,128)} %get-tuple-element.12) | data formatting | bytes 1048576
  85.0 2.3 %copy.15 = f32[1024,256]{1,0:T(8,128)} copy(f32[1024,256]{1,0:T(8,128)} %get-tuple-element.13) | data formatting | bytes 2097152
  (1 shorter events, 0.0 us)
where the time goes:
time: 87.6 us; the launch traced here: 87.2 us
  Pallas kernels  79 us (90%)
  local copies, waits for them, and re-layouts  5.41 us (6%)
  other arithmetic  2.2 us (3%)
    pallas_call x1, Pallas kernels, shards(): pl.pallas_call(functools.partial(exchange, dims), out_shape=(jax.ShapeDty...  66.8 us
    pallas_call x1, Pallas kernels, shards(): pl.pallas_call(functools.partial(prepare, dims), out_shape=(jax.ShapeDtyp...  12.2 us
    unnamed x5, local copies, waits for them, and re-layouts  5.31 us

commit v1 on v0

v1 whole, which is shorter than its diff:
```python
import functools

import jax
import jax.numpy as jnp
from jax import lax
from jax.experimental import pallas as pl
from jax.experimental.pallas import tpu as pltpu
from jax.sharding import PartitionSpec as P

MESH = pl.DeviceIdType.MESH
LANES = 128
BLOCK = 256
WINDOW = 48
F32 = jnp.float32
BF16 = jnp.bfloat16
I32 = jnp.int32
PREPARE_VMEM = 24 << 20
EXCHANGE_VMEM = 24 << 20
FINISH_VMEM = 16 << 20


def iota(shape, axis):
    return lax.broadcasted_iota(I32, shape, axis)


def onehot(mask):
    return jnp.where(mask, 1.0, 0.0).astype(BF16)


def dot(a, b):
    return jnp.dot(a, b, preferred_element_type=F32)


def halves(x):
    high = x.astype(BF16)
    low = (x - high.astype(F32)).astype(BF16)
    return jnp.concatenate([high, low], axis=1)


def prepare(
    dims, kern_hbm, thermal_hbm, kinetic_hbm, slot_hbm, tile_hbm, owner_hbm,
    out_ref, rank_ref, kern_ref, slot_smem, thermal_ref, kinetic_ref, slot_ref, tile_ref, owner_ref,
    thermal32, kinetic32, part_ref, split_ref, sems, small_sem,
):
    vol_count, pix_count, slots, block_tiles, bucket = dims
    entries = kern_ref.shape[0]
    blocks = entries // BLOCK
    pieces = sems.shape[0]
    piece = entries // pieces
    lines = BLOCK // LANES

    block_high = block_tiles // LANES
    first_high = pl.multiple_of(lax.axis_index("vol") * block_high, block_high)
    small = [
        pltpu.make_async_copy(tile_hbm, tile_ref, small_sem.at[0]),
        pltpu.make_async_copy(owner_hbm.at[pl.ds(first_high, block_high)], owner_ref, small_sem.at[1]),
        pltpu.make_async_copy(slot_hbm, slot_smem, small_sem.at[2]),
        pltpu.make_async_copy(slot_hbm, slot_ref, small_sem.at[3]),
        pltpu.make_async_copy(thermal_hbm, thermal_ref, small_sem.at[4]),
        pltpu.make_async_copy(kinetic_hbm, kinetic_ref, small_sem.at[5]),
    ]
    for copy in small:
        copy.start()

    def fetch(q):
        rows = pl.ds(q * piece, piece)
        return pltpu.make_async_copy(kern_hbm.at[rows], kern_ref.at[rows], sems.at[q])

    for q in range(pieces):
        fetch(q).start()

    small[0].wait()
    small[1].wait()
    mine = owner_ref[...] == lax.axis_index("pix")
    ones = jnp.where(mine, 1.0, 0.0)
    upper = onehot(iota((LANES, LANES), 0) < iota((LANES, LANES), 1))
    above = onehot(iota((block_high, block_high), 1) < iota((block_high, block_high), 0))
    total = jnp.broadcast_to(jnp.sum(ones, axis=1, keepdims=True), (block_high, LANES))
    rank = dot(ones.astype(BF16), upper) + dot(above, total.astype(BF16))
    rank_ref[...] = jnp.where(mine, rank, -1.0).astype(I32)

    tile = tile_ref[...]
    block, low = tile // block_tiles, tile % block_tiles
    to_block = iota((vol_count, slots), 0) == block
    ones = jnp.where(to_block, 1.0, 0.0)
    carry = jnp.zeros((vol_count, 1), F32)
    position = []
    for j in range(slots // LANES):
        chunk = ones[:, j * LANES:(j + 1) * LANES]
        ranks = dot(chunk.astype(BF16), upper) + carry
        position.append(jnp.sum(chunk * ranks, axis=0, keepdims=True))
        carry = carry + jnp.sum(chunk, axis=1, keepdims=True)
    position = jnp.concatenate(position, axis=1).astype(I32)
    place = block * bucket + position

    places = onehot(iota((bucket, slots), 0) == position)
    row_high, row_low = (low // 256).astype(F32), (low % 256 + 1).astype(F32)
    values = jnp.concatenate(
        [jnp.where(to_block, row_high, 0.0), jnp.where(to_block, row_low, 0.0)], axis=0
    )
    placed = lax.dot_general(
        values.astype(BF16), places, (((1,), (1,)), ((), ())), preferred_element_type=F32
    )
    rows = placed[:vol_count] * 256.0 + placed[vol_count:] - 1.0
    for b in range(vol_count):
        names = [rows[b:b + 1, q * LANES:(q + 1) * LANES] for q in range(bucket // LANES)]
        names = jnp.concatenate(names + [jnp.zeros((8 - len(names), LANES), F32)], axis=0)
        for c in range(2):
            out_ref[b, c, bucket:bucket + 8, :] = names

    part_ref[...] = jnp.zeros_like(part_ref)
    within = iota((WINDOW, BLOCK), 0)
    for copy in small[2:]:
        copy.wait()
    thermal32[...] = thermal_ref[...].astype(F32)
    kinetic32[...] = kinetic_ref[...].astype(F32)

    def base_of(i):
        return slot_smem[lines * i, 0] // 8 * 8

    def add_window(i, base):
        def pair(ref):
            return jnp.concatenate([ref[pl.ds(lines * i + j, 1), :] for j in range(lines)], axis=1)

        base = pl.multiple_of(base, 8)
        match = within + base == pair(slot_ref)
        weights = jnp.concatenate(
            [jnp.where(match, pair(thermal32), 0.0), jnp.where(match, pair(kinetic32), 0.0)], axis=0
        ).astype(BF16)
        sums = dot(weights, kern_ref[pl.ds(pl.multiple_of(i * BLOCK, BLOCK), BLOCK), :])
        part_ref[pl.ds(base, WINDOW), 0:LANES] += sums[:WINDOW]
        part_ref[pl.ds(base, WINDOW), LANES:2 * LANES] += sums[WINDOW:]

    per = blocks // pieces
    for q in range(pieces):
        fetch(q).wait()

        def first_window(i, unused):
            add_window(i, base_of(i))
            return unused

        lax.fori_loop(q * per, (q + 1) * per, first_window, 0, unroll=4)

    def more_windows(i, unused):
        base = base_of(i)
        extra = (slot_smem[lines * i + lines - 1, LANES - 1] - base) // WINDOW

        def one(w, unused):
            add_window(i, base + w * WINDOW)
            return unused

        return lax.fori_loop(1, extra + 1, one, unused)

    lax.fori_loop(0, blocks, more_windows, 0)

    split_ref[...] = halves(part_ref[0:slots, :])

    def permute(b, unused):
        moved = dot(onehot(iota((bucket, slots), 0) + b * bucket == place), split_ref[...])
        for c in range(2):
            high, low = c * LANES, (c + 2) * LANES
            out_ref[b, c, 0:bucket, :] = moved[:, high:high + LANES] + moved[:, low:low + LANES]
        return unused

    lax.fori_loop(0, vol_count, permute, 0)


def exchange(
    dims, out_hbm, gathered, arrived, sums_ref, swapped, sums, crossed,
    send_sem, recv_sem, local_sem, swap_send, swap_recv, mid_send, mid_recv, own_send, own_recv,
    far_send, far_recv, pass_send, pass_recv,
):
    vol_count, pix_count, block_tiles, bucket = dims
    half = vol_count // 2
    near_count = 2 * half
    members = pix_count // 2
    share = block_tiles // members
    vol, pix = lax.axis_index("vol"), lax.axis_index("pix")
    side, place = vol // half, vol % half
    chip, core = pix // 2, pix % 2
    group, channel = chip // 2, chip % 2
    member = group * 2 + core
    across = (vol + half) % vol_count
    mine = place * 2 + channel

    def peer(k):
        return (place + k // 2) % half, (channel + k % 2) % 2

    def pix_of(other_group, other_channel, other_core):
        return (other_group * 2 + other_channel) * 2 + other_core

    barrier = pltpu.get_barrier_semaphore()

    def signal(other_vol, other_pix):
        pl.semaphore_signal(
            barrier, inc=1, device_id=(other_vol, other_pix), device_id_type=MESH
        )

    def greet_near(k, unused):
        other_place, other_channel = peer(k)
        signal(side * half + other_place, pix_of(group, other_channel, core))
        return unused

    signal(across, pix)
    for k in range(1, pix_count):
        signal(vol, (pix + k) % pix_count)
    lax.fori_loop(2, near_count, greet_near, 0)
    pl.semaphore_wait(barrier, near_count - 2 + pix_count)

    def final(stage, other_place):
        return (side * half + other_place + half * (1 - stage)) % vol_count

    def rows_copy(stage, k):
        other_place, other_channel = peer(k)
        return pltpu.make_async_remote_copy(
            src_ref=out_hbm.at[final(stage, other_place), other_channel],
            dst_ref=arrived.at[stage, mine],
            send_sem=send_sem.at[stage, k], recv_sem=recv_sem.at[stage, k],
            device_id=(side * half + other_place, pix_of(group, other_channel, core)),
            device_id_type=MESH,
        )

    def local_copy(stage):
        return pltpu.make_async_copy(
            out_hbm.at[final(stage, place), channel], arrived.at[stage, mine], local_sem.at[stage]
        )

    for stage in range(2):

        def send(k, unused):
            rows_copy(stage, k).start()
            return unused

        local_copy(stage).start()
        lax.fori_loop(1, near_count, send, 0)

    def sum_up(stage):
        target = sums_ref.at[stage]
        local_copy(stage).wait()
        target[...] = jnp.zeros((block_tiles, LANES), F32)

        def receive(i, unused):
            def one(j, unused):
                rows_copy(stage, 2 * i + j).wait_recv()
                return unused

            lax.fori_loop(jnp.where(i == 0, 1, 0), 2, one, 0)
            sender = (place + half - i) % half * 2
            names, values = [], []
            for j in range(2):
                for q in range(bucket // LANES):
                    names.append(arrived[stage, sender + j, bucket + q:bucket + q + 1, :])
                values.append(arrived[stage, sender + j, 0:bucket, :])
            names = jnp.concatenate(names, axis=1).astype(I32)
            places = onehot(iota((block_tiles, 2 * bucket), 0) == names)
            moved = dot(places, halves(jnp.concatenate(values, axis=0)))
            target[...] += moved[:, :LANES] + moved[:, LANES:]
            return unused

        lax.fori_loop(0, half, receive, 0)

    def swap_copy(stage, k):
        other = (member + k) % members
        return pltpu.make_async_remote_copy(
            src_ref=sums_ref.at[stage, pl.ds(other * share, share)],
            dst_ref=swapped.at[stage, k - 1],
            send_sem=swap_send.at[stage, k], recv_sem=swap_recv.at[stage, k],
            device_id=(vol, pix_of(other // 2, channel, other % 2)), device_id_type=MESH,
        )

    piece_count = mid_send.shape[0]
    piece_rows = share // piece_count

    def part(q):
        return pl.ds(q * piece_rows, piece_rows)

    def reduced(stage, q):
        rows = pl.ds(pl.multiple_of(member * share + q * piece_rows, piece_rows), piece_rows)
        value = sums_ref[stage, rows, :]
        for k in range(1, members):
            value = value + swapped[stage, k - 1, part(q), :]
        return value

    def mid_copy(q):
        return pltpu.make_async_remote_copy(
            src_ref=sums.at[part(q)], dst_ref=crossed.at[part(q)],
            send_sem=mid_send.at[q], recv_sem=mid_recv.at[q],
            device_id=(across, pix), device_id_type=MESH,
        )

    for stage in range(2):
        sum_up(stage)
        for k in range(1, members):
            swap_copy(stage, k).start()
        for k in range(1, members):
            swap_copy(stage, k).wait_recv()
        if stage == 0:
            for q in range(piece_count):
                sums[part(q), :] = reduced(0, q)
                mid_copy(q).start()

    sibling = (vol, pix - core + (1 - core))
    others = range(1, pix_count // 2)

    def far_copy(k, q):
        return pltpu.make_async_remote_copy(
            src_ref=gathered.at[pix, part(q)], dst_ref=gathered.at[pix, part(q)],
            send_sem=far_send.at[k, q], recv_sem=far_recv.at[k, q],
            device_id=(vol, (pix + 2 * k) % pix_count), device_id_type=MESH,
        )

    def pass_copy(k, q):
        source = (pix + pix_count - 2 * k) % pix_count
        return pltpu.make_async_remote_copy(
            src_ref=gathered.at[source, part(q)], dst_ref=gathered.at[source, part(q)],
            send_sem=pass_send.at[k, q], recv_sem=pass_recv.at[k, q],
            device_id=sibling, device_id_type=MESH,
        )

    def own_copy(q):
        return pltpu.make_async_remote_copy(
            src_ref=gathered.at[pix, part(q)], dst_ref=gathered.at[pix, part(q)],
            send_sem=own_send.at[q], recv_sem=own_recv.at[q],
            device_id=sibling, device_id_type=MESH,
        )

    def relay(q):
        for k in others:
            far_copy(k, q).wait_recv()
            pass_copy(k, q).start()

    for q in range(piece_count):
        mid_copy(q).wait_recv()
        gathered[pix, part(q), :] = reduced(1, q) + crossed[part(q), :]
        for k in others:
            far_copy(k, q).start()
        own_copy(q).start()
        if q:
            relay(q - 1)
    relay(piece_count - 1)
    for q in range(piece_count):
        own_copy(q).wait()
        mid_copy(q).wait_send()
        for k in others:
            far_copy(k, q).wait_send()
            pass_copy(k, q).wait()

    for stage in range(2):
        for k in range(1, members):
            swap_copy(stage, k).wait_send()

        def sent(k, unused):
            rows_copy(stage, k).wait_send()
            return unused

        lax.fori_loop(1, near_count, sent, 0)


def finish(gathered, rank_ref, owned_hbm, shell_hbm, split_ref, owned_ref, shell_sem, owned_sem):
    pix_count, share = gathered.shape[0], gathered.shape[1]
    owned_most = owned_ref.shape[0]
    block_tiles = rank_ref.shape[0] * LANES
    copies = []
    for p in range(pix_count):
        chip, core = p // 2, p % 2
        start, channel = (chip // 2 * 2 + core) * share, chip % 2
        copy = pltpu.make_async_copy(
            gathered.at[p],
            shell_hbm.at[pl.ds(start, share), pl.ds(channel * LANES, LANES)],
            shell_sem.at[p],
        )
        copy.start()
        copies.append(copy)
        both = halves(gathered[p])
        for part in range(2):
            first = (2 * part + channel) * LANES
            split_ref[start:start + share, first:first + LANES] = both[:, part * LANES:(part + 1) * LANES]
    rank = jnp.concatenate([rank_ref[q:q + 1, :] for q in range(rank_ref.shape[0])], axis=1)
    moved = dot(onehot(iota((owned_most, block_tiles), 0) == rank), split_ref[...])
    owned_ref[...] = moved[:, :2 * LANES] + moved[:, 2 * LANES:]
    copy = pltpu.make_async_copy(owned_ref, owned_hbm, owned_sem)
    copy.start()
    for other in copies + [copy]:
        other.wait()


def shards(kernel, pressure, velocity, entry_slot, slot_tile, tile_owner):
    vol_count, pix_count = lax.axis_size("vol"), lax.axis_size("pix")
    device_count = vol_count * pix_count
    entries = kernel.shape[0]
    slots = slot_tile.shape[1]
    tiles = tile_owner.shape[0]
    block_tiles = tiles // vol_count
    owned_most = 2 * block_tiles // pix_count
    bucket = 2 * slots // vol_count
    width = 2 * kernel.shape[1]
    vmem = pl.BlockSpec(memory_space=pltpu.VMEM)
    anywhere = pl.BlockSpec(memory_space=pl.ANY)
    hbm = pl.BlockSpec(memory_space=pltpu.HBM)
    dma = pltpu.SemaphoreType.DMA

    shape = (entries // LANES, LANES)
    outgoing, rank = pl.pallas_call(
        functools.partial(prepare, (vol_count, pix_count, slots, block_tiles, bucket)),
        out_shape=(
            jax.ShapeDtypeStruct((vol_count, 2, bucket + 8, LANES), F32),
            jax.ShapeDtypeStruct((block_tiles // LANES, LANES), I32),
        ),
        in_specs=[hbm] * 6,
        out_specs=(vmem, vmem),
        scratch_shapes=[
            pltpu.VMEM(kernel.shape, BF16),
            pltpu.SMEM(shape, I32),
            pltpu.VMEM(shape, BF16),
            pltpu.VMEM(shape, BF16),
            pltpu.VMEM(shape, I32),
            pltpu.VMEM((1, slots), I32),
            pltpu.VMEM((block_tiles // LANES, LANES), I32),
            pltpu.VMEM(shape, F32),
            pltpu.VMEM(shape, F32),
            pltpu.VMEM((slots + WINDOW, width), F32),
            pltpu.VMEM((slots, 2 * width), BF16),
            dma((4,)),
            dma((6,)),
        ],
        compiler_params=pltpu.CompilerParams(vmem_limit_bytes=PREPARE_VMEM),
        name="prepare",
    )(*[
        pltpu.with_memory_space_constraint(x, pltpu.HBM) for x in (
            kernel, pressure.reshape(shape), velocity.reshape(shape), entry_slot.reshape(shape),
            slot_tile, tile_owner.reshape(tiles // LANES, LANES),
        )
    ])

    pieces = 4
    chips = pix_count // 2
    near = vol_count
    share = block_tiles // chips
    gathered = pl.pallas_call(
        functools.partial(exchange, (vol_count, pix_count, block_tiles, bucket)),
        out_shape=jax.ShapeDtypeStruct((pix_count, share, LANES), F32),
        in_specs=[anywhere],
        out_specs=vmem,
        scratch_shapes=[
            pltpu.VMEM((2, near, bucket + 8, LANES), F32),
            pltpu.VMEM((2, block_tiles, LANES), F32),
            pltpu.VMEM((2, chips - 1, share, LANES), F32),
            pltpu.VMEM((share, LANES), F32),
            pltpu.VMEM((share, LANES), F32),
            dma((2, near)), dma((2, near)), dma((2,)), dma((2, chips)), dma((2, chips)),
            dma((pieces,)), dma((pieces,)), dma((pieces,)), dma((pieces,)),
            dma((chips, pieces)), dma((chips, pieces)), dma((chips, pieces)), dma((chips, pieces)),
        ],
        compiler_params=pltpu.CompilerParams(
            collective_id=0, has_side_effects=True, vmem_limit_bytes=EXCHANGE_VMEM
        ),
        name="exchange",
    )(outgoing)

    return pl.pallas_call(
        finish,
        out_shape=(
            jax.ShapeDtypeStruct((owned_most, width), F32),
            jax.ShapeDtypeStruct((block_tiles, width), F32),
        ),
        in_specs=[vmem, vmem],
        out_specs=(anywhere, anywhere),
        scratch_shapes=[
            pltpu.VMEM((block_tiles, 2 * width), BF16),
            pltpu.VMEM((owned_most, width), F32),
            dma((pix_count,)),
            dma,
        ],
        compiler_params=pltpu.CompilerParams(vmem_limit_bytes=FINISH_VMEM),
        name="finish",
    )(gathered, rank)


def solution(mesh):
    in_specs = (
        P(("vol", "pix"), None),
        P(("vol", "pix")),
        P(("vol", "pix")),
        P(("vol", "pix"), None),
        P(("vol", "pix"), None),
        P(),
    )
    out_specs = (P(("vol", "pix"), None), P("vol", None))
    return jax.shard_map(shards, mesh=mesh, in_specs=in_specs, out_specs=out_specs, check_vma=False)
```

time: 87.6 us -> 59.9 us (0.68)
  the two profiles are of different devices: /device:TPU:29 before, /device:TPU:5 now
where the time goes in v1:
time: 59.9 us; the launch traced here: 59.7 us
  Pallas kernels  59.1 us (99%)
  between operations  0.65 us (1%)
    pallas_call x1, Pallas kernels, shards(): pl.pallas_call(functools.partial(exchange, (vol_count, pix_count, block_t...  46.4 us
    pallas_call x1, Pallas kernels, shards(): pl.pallas_call(functools.partial(prepare, (vol_count, pix_count, slots, b...  11.1 us
    pallas_call x1, Pallas kernels, shards(): pl.pallas_call(finish, out_shape=(jax.ShapeDtypeStruct((owned_most, width...  1.63 us

profile of v1, /device:TPU:5, one launch (start us, length us, event | category | flops | bytes accessed | tf_op | source)
XLA Modules:
  0.0 59.7 jit_solution(9358819166471709811)
XLA Ops:
  0.6 11.1 %prepare.1 = (f32[8,2,264,128]{3,2,1,0:T(8,128)S(1)}, s32[8,128]{1,0:T(8,128)S(1)}) custom-call(bf16[16384,128]{1,0:T(8,128)(2,1)} %kern_hbm.1, bf16[128,128]{1,0:T(8,128)(2,1)} %bitcast.5, bf16[128,128]{1,0:T(8,128)(2,1)} %bitcast.6, s32[128,128]{1,0:T(8,128)} %bitcast.4, s32[1,1024]{1,0:T(1,128)} %tile_hbm.1, s32[64,128]{1,0:T(8,128)} %bitcast.7), custom_call_target="tpu_custom_call" | custom-call | tf_op jit(solution)/shard_map/prepare/pallas_call | solution.py:403
  11.7 46.4 %exchange.1.gathered = f32[4,512,128]{2,1,0:T(8,128)S(1)} custom-call(f32[8,2,264,128]{3,2,1,0:T(8,128)S(1)} %get-tuple-element.4.out_hbm), custom_call_target="tpu_custom_call" | custom-call | tf_op jit(solution)/shard_map/exchange/pallas_call | solution.py:439
  58.1 1.6 %finish.1 = (f32[512,256]{1,0:T(8,128)}, f32[1024,256]{1,0:T(8,128)}) custom-call(f32[4,512,128]{2,1,0:T(8,128)S(1)} %exchange.1.gathered, s32[8,128]{1,0:T(8,128)S(1)} %get-tuple-element.5.rank_ref), custom_call_target="tpu_custom_call" | custom-call | tf_op jit(solution)/shard_map/finish/pallas_call | solution.py:460

commit v2 on v1

v2 whole, which is shorter than its diff:
```python
import functools

import jax
import jax.numpy as jnp
from jax import lax
from jax.experimental import pallas as pl
from jax.experimental.pallas import tpu as pltpu
from jax.sharding import PartitionSpec as P

MESH = pl.DeviceIdType.MESH
LANES = 128
BLOCK = 256
WINDOW = 48
F32 = jnp.float32
BF16 = jnp.bfloat16
I32 = jnp.int32
PREPARE_VMEM = 24 << 20
EXCHANGE_VMEM = 24 << 20
FINISH_VMEM = 16 << 20


def iota(shape, axis):
    return lax.broadcasted_iota(I32, shape, axis)


def onehot(mask):
    return jnp.where(mask, 1.0, 0.0).astype(BF16)


def dot(a, b):
    return jnp.dot(a, b, preferred_element_type=F32)


def halves(x):
    high = x.astype(BF16)
    low = (x - high.astype(F32)).astype(BF16)
    return jnp.concatenate([high, low], axis=1)


def prepare(
    dims, kern_hbm, thermal_hbm, kinetic_hbm, slot_hbm, tile_hbm, owner_hbm,
    out_ref, ids_ref, rank_ref, kern_ref, slot_smem, thermal_ref, kinetic_ref, slot_ref, tile_ref, owner_ref,
    thermal32, kinetic32, part_ref, split_ref, sems, small_sem,
):
    vol_count, pix_count, slots, block_tiles, bucket = dims
    entries = kern_ref.shape[0]
    blocks = entries // BLOCK
    pieces = sems.shape[0]
    piece = entries // pieces
    lines = BLOCK // LANES

    block_high = block_tiles // LANES
    first_high = pl.multiple_of(lax.axis_index("vol") * block_high, block_high)
    small = [
        pltpu.make_async_copy(tile_hbm, tile_ref, small_sem.at[0]),
        pltpu.make_async_copy(owner_hbm.at[pl.ds(first_high, block_high)], owner_ref, small_sem.at[1]),
        pltpu.make_async_copy(slot_hbm, slot_smem, small_sem.at[2]),
        pltpu.make_async_copy(slot_hbm, slot_ref, small_sem.at[3]),
        pltpu.make_async_copy(thermal_hbm, thermal_ref, small_sem.at[4]),
        pltpu.make_async_copy(kinetic_hbm, kinetic_ref, small_sem.at[5]),
    ]
    for copy in small:
        copy.start()

    def fetch(q):
        rows = pl.ds(q * piece, piece)
        return pltpu.make_async_copy(kern_hbm.at[rows], kern_ref.at[rows], sems.at[q])

    for q in range(pieces):
        fetch(q).start()

    small[0].wait()
    small[1].wait()
    mine = owner_ref[...] == lax.axis_index("pix")
    ones = jnp.where(mine, 1.0, 0.0)
    upper = onehot(iota((LANES, LANES), 0) < iota((LANES, LANES), 1))
    above = onehot(iota((block_high, block_high), 1) < iota((block_high, block_high), 0))
    total = jnp.broadcast_to(jnp.sum(ones, axis=1, keepdims=True), (block_high, LANES))
    rank = dot(ones.astype(BF16), upper) + dot(above, total.astype(BF16))
    rank_ref[...] = jnp.where(mine, rank, -1.0).astype(I32)

    half = vol_count // 2
    side = lax.axis_index("vol") // half
    tile = tile_ref[...]
    block, low = tile // block_tiles, tile % block_tiles
    order = (block + vol_count - (1 - side) * half) % vol_count
    to_block = iota((vol_count, slots), 0) == order
    ones = jnp.where(to_block, 1.0, 0.0)
    carry = jnp.zeros((vol_count, 1), F32)
    position = []
    for j in range(slots // LANES):
        chunk = ones[:, j * LANES:(j + 1) * LANES]
        ranks = dot(chunk.astype(BF16), upper) + carry
        position.append(jnp.sum(chunk * ranks, axis=0, keepdims=True))
        carry = carry + jnp.sum(chunk, axis=1, keepdims=True)
    position = jnp.concatenate(position, axis=1)
    starts = [jnp.zeros((1, 1), F32)]
    for b in range(vol_count - 1):
        starts.append(starts[-1] + carry[b:b + 1, :])
    starts = jnp.concatenate(starts, axis=0)
    place = (position + jnp.sum(ones * starts, axis=0, keepdims=True)).astype(I32)

    places = onehot(iota((bucket, slots), 0) == position.astype(I32))
    row_high, row_low = (low // 256).astype(F32), (low % 256 + 1).astype(F32)
    values = jnp.concatenate(
        [jnp.where(to_block, row_high, 0.0), jnp.where(to_block, row_low, 0.0)], axis=0
    )
    placed = lax.dot_general(
        values.astype(BF16), places, (((1,), (1,)), ((), ())), preferred_element_type=F32
    )
    rows = (placed[:vol_count] * 256.0 + placed[vol_count:] - 1.0).astype(I32)
    per_block = bucket // LANES
    names = jnp.concatenate(
        [rows[b:b + 1, q * LANES:(q + 1) * LANES] for b in range(vol_count) for q in range(per_block)],
        axis=0,
    )
    ids_ref[0:vol_count * per_block, :] = names
    on_lane = iota((vol_count, LANES), 0) == iota((vol_count, LANES), 1)
    line = jnp.sum(jnp.where(on_lane, starts, 0.0), axis=0, keepdims=True).astype(I32)
    ids_ref[vol_count * per_block:, :] = jnp.broadcast_to(line, (8, LANES))

    part_ref[...] = jnp.zeros_like(part_ref)
    within = iota((WINDOW, BLOCK), 0)
    for copy in small[2:]:
        copy.wait()
    thermal32[...] = thermal_ref[...].astype(F32)
    kinetic32[...] = kinetic_ref[...].astype(F32)

    def base_of(i):
        return slot_smem[lines * i, 0] // 8 * 8

    def add_window(i, base):
        def pair(ref):
            return jnp.concatenate([ref[pl.ds(lines * i + j, 1), :] for j in range(lines)], axis=1)

        base = pl.multiple_of(base, 8)
        match = within + base == pair(slot_ref)
        weights = jnp.concatenate(
            [jnp.where(match, pair(thermal32), 0.0), jnp.where(match, pair(kinetic32), 0.0)], axis=0
        ).astype(BF16)
        sums = dot(weights, kern_ref[pl.ds(pl.multiple_of(i * BLOCK, BLOCK), BLOCK), :])
        part_ref[pl.ds(base, WINDOW), 0:LANES] += sums[:WINDOW]
        part_ref[pl.ds(base, WINDOW), LANES:2 * LANES] += sums[WINDOW:]

    per = blocks // pieces
    for q in range(pieces):
        fetch(q).wait()

        def first_window(i, unused):
            add_window(i, base_of(i))
            return unused

        lax.fori_loop(q * per, (q + 1) * per, first_window, 0, unroll=4)

    def more_windows(i, unused):
        base = base_of(i)
        extra = (slot_smem[lines * i + lines - 1, LANES - 1] - base) // WINDOW

        def one(w, unused):
            add_window(i, base + w * WINDOW)
            return unused

        return lax.fori_loop(1, extra + 1, one, unused)

    lax.fori_loop(0, blocks, more_windows, 0)

    split_ref[...] = halves(part_ref[0:slots, :])

    cols, sub = LANES // half, bucket // half
    lane = iota((sub, LANES), 1) // cols

    def permute(q, unused):
        moved = dot(onehot(iota((bucket, slots), 0) + q * bucket == place), split_ref[...])
        for c in range(2):
            high, low = c * LANES, (c + 2) * LANES
            value = moved[:, high:high + LANES] + moved[:, low:low + LANES]
            rolled = [value] + [pltpu.roll(value, d * cols, 1) for d in range(1, half)]
            for h in range(half):
                packed = rolled[(half - h) % half][0:sub]
                for u in range(1, half):
                    packed = jnp.where(
                        lane == u, rolled[(u - h) % half][u * sub:(u + 1) * sub], packed
                    )
                out_ref[h, c, q] = packed
        return unused

    lax.fori_loop(0, half, permute, 0)


def exchange(
    dims, out_hbm, ids_hbm, gathered, arrived, ids, starts, rows_ref, acc, partial, swapped, sums,
    crossed, total, send_sem, recv_sem, ids_send, ids_recv, local_sem, start_sem, swap_send,
    swap_recv, mid_send, mid_recv, far_send, far_recv, own_sem, pass_send, pass_recv,
):
    vol_count, pix_count, block_tiles, bucket = dims
    half = vol_count // 2
    near_count = 2 * half
    chips = pix_count // 2
    members = chips
    cols, sub = LANES // half, bucket // half
    group_tiles = block_tiles // half
    share = group_tiles // members
    per_block = bucket // LANES
    vol, pix = lax.axis_index("vol"), lax.axis_index("pix")
    side, place = vol // half, vol % half
    chip, core = pix // 2, pix % 2
    group, channel = chip // 2, chip % 2
    member = group * 2 + core
    across = (vol + half) % vol_count
    mine = place * 2 + channel
    sibling = (vol, pix - core + (1 - core))

    def peer(k):
        return (place + k // 2) % half, (channel + k % 2) % 2

    def sender(k):
        return (place + half - k // 2) % half * 2 + (channel + k % 2) % 2

    def pix_of(other_group, other_channel, other_core):
        return (other_group * 2 + other_channel) * 2 + other_core

    barrier = pltpu.get_barrier_semaphore()

    def signal(other_vol, other_pix):
        pl.semaphore_signal(
            barrier, inc=1, device_id=(other_vol, other_pix), device_id_type=MESH
        )

    def greet(k, unused):
        signal(side * half + (place + k // chips) % half, (chip + k % chips) % chips * 2 + core)
        return unused

    signal(across, pix)
    for k in range(1, pix_count):
        signal(vol, (pix + k) % pix_count)
    lax.fori_loop(chips, half * chips, greet, 0)
    pl.semaphore_wait(barrier, pix_count + (half - 1) * chips)

    def target(k):
        other_place, other_channel = peer(k)
        return side * half + other_place, pix_of(group, other_channel, core)

    def rows_copy(q, k):
        other_place, other_channel = peer(k)
        return pltpu.make_async_remote_copy(
            src_ref=out_hbm.at[other_place, other_channel, q], dst_ref=arrived.at[q, mine],
            send_sem=send_sem.at[q, k], recv_sem=recv_sem.at[q, k],
            device_id=target(k), device_id_type=MESH,
        )

    def ids_copy(k):
        return pltpu.make_async_remote_copy(
            src_ref=ids_hbm, dst_ref=ids.at[mine],
            send_sem=ids_send.at[k], recv_sem=ids_recv.at[k],
            device_id=target(k), device_id_type=MESH,
        )

    def local_rows(q):
        return pltpu.make_async_copy(
            out_hbm.at[place, channel, q], arrived.at[q, mine], local_sem.at[q]
        )

    local_ids = pltpu.make_async_copy(ids_hbm, ids.at[mine], local_sem.at[half])

    def send_ids(k, unused):
        ids_copy(k).start()
        return unused

    lax.fori_loop(1, near_count, send_ids, 0)
    local_ids.start()

    def send_chunk(q, unused):
        def one(k, unused):
            rows_copy(q, k).start()
            return unused

        lax.fori_loop(1, near_count, one, 0)
        local_rows(q).start()
        return unused

    lax.fori_loop(0, half, send_chunk, 0)

    def clear(s, unused):
        rows_ref[s, half * bucket:(half + 1) * bucket, :] = jnp.zeros((bucket, LANES), F32)
        return unused

    lax.fori_loop(0, near_count, clear, 0)

    def start_copy(s):
        return pltpu.make_async_copy(
            ids.at[s, pl.ds(vol_count * per_block, 1)], starts.at[pl.ds(s, 1)], start_sem.at[s]
        )

    local_ids.wait()
    start_copy(mine).start()

    def take_ids(k, unused):
        ids_copy(k).wait_recv()
        start_copy(sender(k)).start()
        return unused

    lax.fori_loop(1, near_count, take_ids, 0)

    def take_starts(s, unused):
        start_copy(s).wait()
        return unused

    lax.fori_loop(0, near_count, take_starts, 0)

    lane = iota((1, LANES), 1) // cols
    wide = iota((sub, LANES), 1) // cols

    def unpack(q, s):
        value = arrived[q, s]
        rolled = [value] + [pltpu.roll(value, d * cols, 1) for d in range(1, half)]
        for u in range(half):
            spread = rolled[(half - u) % half]
            for v in range(1, half):
                spread = jnp.where(wide == v, rolled[(v - u) % half], spread)
            first = pl.multiple_of(q * bucket + u * sub, sub)
            rows_ref[s, pl.ds(first, sub), :] = spread

    def accumulate(b, s):
        both = halves(rows_ref[s, pl.ds(starts[s, b], bucket), :])
        names = jnp.concatenate(
            [ids[s, pl.ds(b * per_block + j, 1), :] for j in range(per_block)], axis=1
        )
        tile = iota((group_tiles, bucket), 0)
        places, values = [], []
        for u in range(half):
            places.append(onehot(tile + u * group_tiles == names))
            keep = onehot(lane == u)
            values.append(both * jnp.concatenate([keep, keep], axis=1))
        acc[...] += dot(jnp.concatenate(places, axis=1), jnp.concatenate(values, axis=0))

    def swap_copy(b, k):
        other = (member + k) % members
        return pltpu.make_async_remote_copy(
            src_ref=partial.at[b, pl.ds(other * share, share)], dst_ref=swapped.at[b, k - 1],
            send_sem=swap_send.at[b, k], recv_sem=swap_recv.at[b, k],
            device_id=(vol, pix_of(other // 2, channel, other % 2)), device_id_type=MESH,
        )

    def swap(b):
        partial[b] = acc[:, :LANES] + acc[:, LANES:]
        for k in range(1, members):
            swap_copy(b, k).start()

    def reduced(b):
        for k in range(1, members):
            swap_copy(b, k).wait_recv()
        value = partial[b, pl.ds(pl.multiple_of(member * share, share), share), :]
        for k in range(1, members):
            value = value + swapped[b, k - 1]
        return value

    def mid_copy(b):
        return pltpu.make_async_remote_copy(
            src_ref=sums.at[b], dst_ref=crossed.at[b],
            send_sem=mid_send.at[b], recv_sem=mid_recv.at[b],
            device_id=(across, pix), device_id_type=MESH,
        )

    def far(q, unused):
        acc[...] = jnp.zeros(acc.shape, F32)
        local_rows(q).wait()
        unpack(q, mine)
        accumulate(q, mine)

        def one(k, unused):
            rows_copy(q, k).wait_recv()
            unpack(q, sender(k))
            accumulate(q, sender(k))
            return unused

        lax.fori_loop(1, near_count, one, 0)
        swap(q)
        sums[q] = reduced(q)
        mid_copy(q).start()
        return unused

    lax.fori_loop(0, half, far, 0)

    def off(i):
        return (i + half - place) % half

    def far_copy(i, k):
        return pltpu.make_async_remote_copy(
            src_ref=total.at[i], dst_ref=gathered.at[core, place, chip],
            send_sem=far_send.at[off(i), k], recv_sem=far_recv.at[off(i), k],
            device_id=(side * half + i, (chip + k) % chips * 2 + core), device_id_type=MESH,
        )

    def own_copy():
        return pltpu.make_async_copy(total.at[place], gathered.at[core, place, chip], own_sem)

    def finalize(i):
        value = reduced(half + i)
        mid_copy(i).wait_recv()
        total[i] = value + crossed[i]

        @pl.when(i != place)
        def _():
            far_copy(i, 0).start()

        @pl.when(i == place)
        def _():
            own_copy().start()

        for k in range(1, chips):
            far_copy(i, k).start()

    def near(i, unused):
        acc[...] = jnp.zeros(acc.shape, F32)

        def one(s, unused):
            accumulate(half + i, s)
            return unused

        lax.fori_loop(0, near_count, one, 0)
        swap(half + i)

        @pl.when(i > 0)
        def _():
            finalize(i - 1)

        return unused

    lax.fori_loop(0, half, near, 0)
    finalize(half - 1)

    def pass_copy(o, k):
        piece = gathered.at[core, (place + half - o) % half, (chip + chips - k) % chips]
        return pltpu.make_async_remote_copy(
            src_ref=piece, dst_ref=piece,
            send_sem=pass_send.at[o, k], recv_sem=pass_recv.at[o, k],
            device_id=sibling, device_id_type=MESH,
        )

    def far_arrival(o, k):
        return pltpu.make_async_remote_copy(
            src_ref=total.at[0], dst_ref=gathered.at[core, place, chip],
            send_sem=far_send.at[o, k], recv_sem=far_recv.at[o, k],
            device_id=(side * half + (place + o) % half, (chip + k) % chips * 2 + core),
            device_id_type=MESH,
        )

    own_copy().wait()
    pass_copy(0, 0).start()
    for k in range(1, chips):
        far_arrival(0, k).wait_recv()
        pass_copy(0, k).start()

    def relay(o, unused):
        for k in range(chips):
            far_arrival(o, k).wait_recv()
            pass_copy(o, k).start()
        return unused

    lax.fori_loop(1, half, relay, 0)

    def passed(o, unused):
        for k in range(chips):
            pass_copy(o, k).wait()
        return unused

    lax.fori_loop(0, half, passed, 0)
    for k in range(1, chips):
        far_arrival(0, k).wait_send()

    def sent(o, unused):
        for k in range(chips):
            far_arrival(o, k).wait_send()
        return unused

    lax.fori_loop(1, half, sent, 0)

    def sent_rows(k, unused):
        ids_copy(k).wait_send()

        def one(q, unused):
            rows_copy(q, k).wait_send()
            return unused

        lax.fori_loop(0, half, one, 0)
        return unused

    lax.fori_loop(1, near_count, sent_rows, 0)

    def sent_sums(b, unused):
        mid_copy(b).wait_send()
        for k in range(1, members):
            swap_copy(b, k).wait_send()
            swap_copy(half + b, k).wait_send()
        return unused

    lax.fori_loop(0, half, sent_sums, 0)


def finish(
    gathered, rank_ref, owned_hbm, shell_hbm, split_ref, shell_ref, owned_ref, shell_sem, owned_sem,
):
    half, chips, share = gathered.shape[1], gathered.shape[2], gathered.shape[3]
    cols = LANES // half
    owned_most = owned_ref.shape[0]
    block_tiles = shell_ref.shape[0]
    group_tiles = block_tiles // half
    lane = iota((share, LANES), 1) // cols
    for core in range(2):
        for chip in range(chips):
            first, channel = (chip // 2 * 2 + core) * share, chip % 2
            rolled = []
            for s in range(half):
                value = gathered[core, s, chip]
                rolled.append([value] + [pltpu.roll(value, d * cols, 1) for d in range(1, half)])
            for u in range(half):
                value = rolled[0][(half - u) % half]
                for s in range(1, half):
                    value = jnp.where(lane == s, rolled[s][(s - u) % half], value)
                start = u * group_tiles + first
                shell_ref[start:start + share, channel * LANES:(channel + 1) * LANES] = value
                both = halves(value)
                for part in range(2):
                    at = (2 * part + channel) * LANES
                    split_ref[start:start + share, at:at + LANES] = both[:, part * LANES:(part + 1) * LANES]
    shell_copy = pltpu.make_async_copy(shell_ref, shell_hbm, shell_sem)
    shell_copy.start()
    rank = jnp.concatenate([rank_ref[q:q + 1, :] for q in range(rank_ref.shape[0])], axis=1)
    moved = dot(onehot(iota((owned_most, block_tiles), 0) == rank), split_ref[...])
    owned_ref[...] = moved[:, :2 * LANES] + moved[:, 2 * LANES:]
    owned_copy = pltpu.make_async_copy(owned_ref, owned_hbm, owned_sem)
    owned_copy.start()
    shell_copy.wait()
    owned_copy.wait()


def shards(kernel, pressure, velocity, entry_slot, slot_tile, tile_owner):
    vol_count, pix_count = lax.axis_size("vol"), lax.axis_size("pix")
    device_count = vol_count * pix_count
    entries = kernel.shape[0]
    slots = slot_tile.shape[1]
    tiles = tile_owner.shape[0]
    block_tiles = tiles // vol_count
    owned_most = 2 * block_tiles // pix_count
    bucket = 2 * slots // vol_count
    width = 2 * kernel.shape[1]
    vmem = pl.BlockSpec(memory_space=pltpu.VMEM)
    anywhere = pl.BlockSpec(memory_space=pl.ANY)
    hbm = pl.BlockSpec(memory_space=pltpu.HBM)
    dma = pltpu.SemaphoreType.DMA

    shape = (entries // LANES, LANES)
    half = vol_count // 2
    sub = bucket // half
    id_rows = vol_count * bucket // LANES + 8
    outgoing, ids, rank = pl.pallas_call(
        functools.partial(prepare, (vol_count, pix_count, slots, block_tiles, bucket)),
        out_shape=(
            jax.ShapeDtypeStruct((half, 2, half, sub, LANES), F32),
            jax.ShapeDtypeStruct((id_rows, LANES), I32),
            jax.ShapeDtypeStruct((block_tiles // LANES, LANES), I32),
        ),
        in_specs=[hbm] * 6,
        out_specs=(vmem, vmem, vmem),
        scratch_shapes=[
            pltpu.VMEM(kernel.shape, BF16),
            pltpu.SMEM(shape, I32),
            pltpu.VMEM(shape, BF16),
            pltpu.VMEM(shape, BF16),
            pltpu.VMEM(shape, I32),
            pltpu.VMEM((1, slots), I32),
            pltpu.VMEM((block_tiles // LANES, LANES), I32),
            pltpu.VMEM(shape, F32),
            pltpu.VMEM(shape, F32),
            pltpu.VMEM((slots + WINDOW, width), F32),
            pltpu.VMEM((slots, 2 * width), BF16),
            dma((4,)),
            dma((6,)),
        ],
        compiler_params=pltpu.CompilerParams(vmem_limit_bytes=PREPARE_VMEM),
        name="prepare",
    )(*[
        pltpu.with_memory_space_constraint(x, pltpu.HBM) for x in (
            kernel, pressure.reshape(shape), velocity.reshape(shape), entry_slot.reshape(shape),
            slot_tile, tile_owner.reshape(tiles // LANES, LANES),
        )
    ])

    chips = pix_count // 2
    near = vol_count
    group_tiles = block_tiles // half
    share = group_tiles // chips
    gathered = pl.pallas_call(
        functools.partial(exchange, (vol_count, pix_count, block_tiles, bucket)),
        out_shape=jax.ShapeDtypeStruct((2, half, chips, share, LANES), F32),
        in_specs=[anywhere, anywhere],
        out_specs=vmem,
        scratch_shapes=[
            pltpu.VMEM((half, near, sub, LANES), F32),
            pltpu.VMEM((near, id_rows, LANES), I32),
            pltpu.SMEM((near, LANES), I32),
            pltpu.VMEM((near, (half + 1) * bucket, LANES), F32),
            pltpu.VMEM((group_tiles, 2 * LANES), F32),
            pltpu.VMEM((vol_count, group_tiles, LANES), F32),
            pltpu.VMEM((vol_count, chips - 1, share, LANES), F32),
            pltpu.VMEM((half, share, LANES), F32),
            pltpu.VMEM((half, share, LANES), F32),
            pltpu.VMEM((half, share, LANES), F32),
            dma((half, near)), dma((half, near)), dma((near,)), dma((near,)),
            dma((half + 1,)), dma((near,)), dma((vol_count, chips)), dma((vol_count, chips)),
            dma((half,)), dma((half,)), dma((half, chips)), dma((half, chips)), dma,
            dma((half, chips)), dma((half, chips)),
        ],
        compiler_params=pltpu.CompilerParams(
            collective_id=0, has_side_effects=True, vmem_limit_bytes=EXCHANGE_VMEM
        ),
        name="exchange",
    )(outgoing, ids)

    return pl.pallas_call(
        finish,
        out_shape=(
            jax.ShapeDtypeStruct((owned_most, width), F32),
            jax.ShapeDtypeStruct((block_tiles, width), F32),
        ),
        in_specs=[vmem, vmem],
        out_specs=(anywhere, anywhere),
        scratch_shapes=[
            pltpu.VMEM((block_tiles, 2 * width), BF16),
            pltpu.VMEM((block_tiles, width), F32),
            pltpu.VMEM((owned_most, width), F32),
            dma,
            dma,
        ],
        compiler_params=pltpu.CompilerParams(vmem_limit_bytes=FINISH_VMEM),
        name="finish",
    )(gathered, rank)


def solution(mesh):
    in_specs = (
        P(("vol", "pix"), None),
        P(("vol", "pix")),
        P(("vol", "pix")),
        P(("vol", "pix"), None),
        P(("vol", "pix"), None),
        P(),
    )
    out_specs = (P(("vol", "pix"), None), P("vol", None))
    return jax.shard_map(shards, mesh=mesh, in_specs=in_specs, out_specs=out_specs, check_vma=False)
```

time: 59.9 us -> 60.7 us (1.013)
  the two profiles are of different devices: /device:TPU:5 before, /device:TPU:29 now
where the time goes in v2:
time: 60.7 us; the launch traced here: 60.1 us
  Pallas kernels  59.5 us (98%)
  between operations  0.65 us (1%)
    pallas_call x1, Pallas kernels, shards(): pl.pallas_call(functools.partial(exchange, (vol_count, pix_count, block_t...  46.9 us
    pallas_call x1, Pallas kernels, shards(): pl.pallas_call(functools.partial(prepare, (vol_count, pix_count, slots, b...  10.2 us
    pallas_call x1, Pallas kernels, shards(): pl.pallas_call(finish, out_shape=(jax.ShapeDtypeStruct((owned_most, width...  2.38 us

profile of v2, /device:TPU:29, one launch (start us, length us, event | category | flops | bytes accessed | tf_op | source)
XLA Modules:
  0.0 60.1 jit_solution(16133545262851979657)
XLA Ops:
  0.6 10.2 %prepare.1 = (f32[4,2,4,64,128]{4,3,2,1,0:T(8,128)S(1)}, s32[24,128]{1,0:T(8,128)S(1)}, s32[8,128]{1,0:T(8,128)S(1)}) custom-call(bf16[16384,128]{1,0:T(8,128)(2,1)} %kern_hbm.1, bf16[128,128]{1,0:T(8,128)(2,1)} %bitcast.5, bf16[128,128]{1,0:T(8,128)(2,1)} %bitcast.6, s32[128,128]{1,0:T(8,128)} %bitcast.4, s32[1,1024]{1,0:T(1,128)} %tile_hbm.1, ...), custom_call_target="tpu_custom_call" | custom-call | tf_op jit(solution)/shard_map/prepare/pallas_call | solution.py:556
  10.8 46.9 %exchange.1.gathered = f32[2,4,2,128,128]{4,3,2,1,0:T(8,128)S(1)} custom-call(f32[4,2,4,64,128]{4,3,2,1,0:T(8,128)S(1)} %get-tuple-element.5.out_hbm, s32[24,128]{1,0:T(8,128)S(1)} %get-tuple-element.6.ids_hbm), custom_call_target="tpu_custom_call" | custom-call | tf_op jit(solution)/shard_map/exchange/pallas_call | solution.py:593
  57.7 2.4 %finish.1 = (f32[512,256]{1,0:T(8,128)}, f32[1024,256]{1,0:T(8,128)}) custom-call(f32[2,4,2,128,128]{4,3,2,1,0:T(8,128)S(1)} %exchange.1.gathered, s32[8,128]{1,0:T(8,128)S(1)} %get-tuple-element.7.rank_ref), custom_call_target="tpu_custom_call" | custom-call | tf_op jit(solution)/shard_map/finish/pallas_call | solution.py:620

commit v3 on v2

--- a/solution.py
+++ b/solution.py
@@ -84,38 +84,40 @@
     tile = tile_ref[...]
     block, low = tile // block_tiles, tile % block_tiles
     order = (block + vol_count - (1 - side) * half) % vol_count
-    to_block = iota((vol_count, slots), 0) == order
-    ones = jnp.where(to_block, 1.0, 0.0)
-    carry = jnp.zeros((vol_count, 1), F32)
+    group_tiles = block_tiles // half
+    kinds = vol_count * half
+    to_kind = iota((kinds, slots), 0) == order * half + low // group_tiles
+    ones = jnp.where(to_kind, 1.0, 0.0)
+    carry = jnp.zeros((kinds, 1), F32)
     position = []
     for j in range(slots // LANES):
         chunk = ones[:, j * LANES:(j + 1) * LANES]
         ranks = dot(chunk.astype(BF16), upper) + carry
         position.append(jnp.sum(chunk * ranks, axis=0, keepdims=True))
         carry = carry + jnp.sum(chunk, axis=1, keepdims=True)
+    counts = jnp.broadcast_to(carry, (kinds, LANES)).astype(BF16)
+    earlier = iota((kinds, kinds), 1) < iota((kinds, kinds), 0)
+    same = iota((kinds, kinds), 1) // half == iota((kinds, kinds), 0) // half
+    starts = dot(onehot(earlier), counts)
+    inner = dot(onehot(earlier & same), counts)
     position = jnp.concatenate(position, axis=1)
-    starts = [jnp.zeros((1, 1), F32)]
-    for b in range(vol_count - 1):
-        starts.append(starts[-1] + carry[b:b + 1, :])
-    starts = jnp.concatenate(starts, axis=0)
-    place = (position + jnp.sum(ones * starts, axis=0, keepdims=True)).astype(I32)
-
-    places = onehot(iota((bucket, slots), 0) == position.astype(I32))
-    row_high, row_low = (low // 256).astype(F32), (low % 256 + 1).astype(F32)
-    values = jnp.concatenate(
-        [jnp.where(to_block, row_high, 0.0), jnp.where(to_block, row_low, 0.0)], axis=0
-    )
-    placed = lax.dot_general(
+    place = (position + jnp.sum(ones * starts[:, 0:1], axis=0, keepdims=True)).astype(I32)
+    position = (position + jnp.sum(ones * inner[:, 0:1], axis=0, keepdims=True)).astype(I32)
+
+    places = onehot(iota((bucket, slots), 0) == position)
+    to_block = iota((vol_count, slots), 0) == order
+    values = jnp.where(to_block, (low % group_tiles + 1).astype(F32), 0.0)
+    rows = lax.dot_general(
         values.astype(BF16), places, (((1,), (1,)), ((), ())), preferred_element_type=F32
     )
-    rows = (placed[:vol_count] * 256.0 + placed[vol_count:] - 1.0).astype(I32)
+    rows = (rows - 1.0).astype(I32)
     per_block = bucket // LANES
     names = jnp.concatenate(
         [rows[b:b + 1, q * LANES:(q + 1) * LANES] for b in range(vol_count) for q in range(per_block)],
         axis=0,
     )
     ids_ref[0:vol_count * per_block, :] = names
-    on_lane = iota((vol_count, LANES), 0) == iota((vol_count, LANES), 1)
+    on_lane = iota((kinds, LANES), 0) == iota((kinds, LANES), 1)
     line = jnp.sum(jnp.where(on_lane, starts, 0.0), axis=0, keepdims=True).astype(I32)
     ids_ref[vol_count * per_block:, :] = jnp.broadcast_to(line, (8, LANES))
 
@@ -209,6 +211,7 @@
     across = (vol + half) % vol_count
     mine = place * 2 + channel
     sibling = (vol, pix - core + (1 - core))
+    id_rows = vol_count * per_block + 1
 
     def peer(k):
         return (place + k // 2) % half, (channel + k % 2) % 2
@@ -250,7 +253,7 @@
 
     def ids_copy(k):
         return pltpu.make_async_remote_copy(
-            src_ref=ids_hbm, dst_ref=ids.at[mine],
+            src_ref=ids_hbm.at[pl.ds(0, id_rows)], dst_ref=ids.at[mine, pl.ds(0, id_rows)],
             send_sem=ids_send.at[k], recv_sem=ids_recv.at[k],
             device_id=target(k), device_id_type=MESH,
         )
@@ -309,6 +312,8 @@
 
     lane = iota((1, LANES), 1) // cols
     wide = iota((sub, LANES), 1) // cols
+    row = iota((bucket, LANES), 0)
+    tile = iota((group_tiles, bucket), 0)
 
     def unpack(q, s):
         value = arrived[q, s]
@@ -320,17 +325,21 @@
             first = pl.multiple_of(q * bucket + u * sub, sub)
             rows_ref[s, pl.ds(first, sub), :] = spread
 
-    def accumulate(b, s):
-        both = halves(rows_ref[s, pl.ds(starts[s, b], bucket), :])
-        names = jnp.concatenate(
-            [ids[s, pl.ds(b * per_block + j, 1), :] for j in range(per_block)], axis=1
-        )
-        tile = iota((group_tiles, bucket), 0)
+    def accumulate(b, senders):
         places, values = [], []
-        for u in range(half):
-            places.append(onehot(tile + u * group_tiles == names))
-            keep = onehot(lane == u)
-            values.append(both * jnp.concatenate([keep, keep], axis=1))
+        for s in senders:
+            first = starts[s, b * half]
+            low, high = jnp.zeros((1, LANES), I32), jnp.full((1, LANES), bucket, I32)
+            for u in range(1, half):
+                bound = starts[s, b * half + u] - first
+                low = jnp.where(lane == u, bound, low)
+                high = jnp.where(lane == u - 1, bound, high)
+            keep = (row >= low) & (row < high)
+            values.append(halves(jnp.where(keep, rows_ref[s, pl.ds(first, bucket), :], 0.0)))
+            names = jnp.concatenate(
+                [ids[s, pl.ds(b * per_block + j, 1), :] for j in range(per_block)], axis=1
+            )
+            places.append(onehot(tile == names))
         acc[...] += dot(jnp.concatenate(places, axis=1), jnp.concatenate(values, axis=0))
 
     def swap_copy(b, k):
@@ -363,17 +372,24 @@
 
     def far(q, unused):
         acc[...] = jnp.zeros(acc.shape, F32)
-        local_rows(q).wait()
-        unpack(q, mine)
-        accumulate(q, mine)
-
-        def one(k, unused):
-            rows_copy(q, k).wait_recv()
-            unpack(q, sender(k))
-            accumulate(q, sender(k))
+
+        def one(p, unused):
+            @pl.when(p == 0)
+            def _():
+                local_rows(q).wait()
+
+            @pl.when(p > 0)
+            def _():
+                rows_copy(q, 2 * p).wait_recv()
+
+            rows_copy(q, 2 * p + 1).wait_recv()
+            senders = [sender(2 * p), sender(2 * p + 1)]
+            for s in senders:
+                unpack(q, s)
+            accumulate(q, senders)
             return unused
 
-        lax.fori_loop(1, near_count, one, 0)
+        lax.fori_loop(0, half, one, 0)
         swap(q)
         sums[q] = reduced(q)
         mid_copy(q).start()
@@ -413,11 +429,11 @@
     def near(i, unused):
         acc[...] = jnp.zeros(acc.shape, F32)
 
-        def one(s, unused):
-            accumulate(half + i, s)
+        def some(p, unused):
+            accumulate(half + i, [4 * p + j for j in range(4)])
             return unused
 
-        lax.fori_loop(0, near_count, one, 0)
+        lax.fori_loop(0, near_count // 4, some, 0)
         swap(half + i)
 
         @pl.when(i > 0)

time: 60.7 us -> 49.8 us (0.82)
  Pallas kernels: 59.5 us -> 48.9 us
    pallas_call x1, Pallas kernels: 46.9 us -> 36.1 us  [shards(): pl.pallas_call(functools.partial(exchange, (vol_count, pix_count, block_t...]
where the time goes in v3:
time: 49.8 us; the launch traced here: 49.5 us
  Pallas kernels  48.9 us (98%)
  between operations  0.65 us (1%)
    pallas_call x1, Pallas kernels, shards(): pl.pallas_call(functools.partial(exchange, (vol_count, pix_count, block_t...  36.1 us
    pallas_call x1, Pallas kernels, shards(): pl.pallas_call(functools.partial(prepare, (vol_count, pix_count, slots, b...  10.4 us
    pallas_call x1, Pallas kernels, shards(): pl.pallas_call(finish, out_shape=(jax.ShapeDtypeStruct((owned_most, width...  2.38 us

profile of v3, /device:TPU:29, one launch (start us, length us, event | category | flops | bytes accessed | tf_op | source)
XLA Modules:
  0.0 49.5 jit_solution(2328351857302912980)
XLA Ops:
  0.6 10.4 %prepare.1 = (f32[4,2,4,64,128]{4,3,2,1,0:T(8,128)S(1)}, s32[24,128]{1,0:T(8,128)S(1)}, s32[8,128]{1,0:T(8,128)S(1)}) custom-call(bf16[16384,128]{1,0:T(8,128)(2,1)} %kern_hbm.1, bf16[128,128]{1,0:T(8,128)(2,1)} %bitcast.5, bf16[128,128]{1,0:T(8,128)(2,1)} %bitcast.6, s32[128,128]{1,0:T(8,128)} %bitcast.4, s32[1,1024]{1,0:T(1,128)} %tile_hbm.1, ...), custom_call_target="tpu_custom_call" | custom-call | tf_op jit(solution)/shard_map/prepare/pallas_call | solution.py:572
  11.0 36.1 %exchange.1.gathered = f32[2,4,2,128,128]{4,3,2,1,0:T(8,128)S(1)} custom-call(f32[4,2,4,64,128]{4,3,2,1,0:T(8,128)S(1)} %get-tuple-element.5.out_hbm, s32[24,128]{1,0:T(8,128)S(1)} %get-tuple-element.6.ids_hbm), custom_call_target="tpu_custom_call" | custom-call | tf_op jit(solution)/shard_map/exchange/pallas_call | solution.py:609
  47.1 2.4 %finish.1 = (f32[512,256]{1,0:T(8,128)}, f32[1024,256]{1,0:T(8,128)}) custom-call(f32[2,4,2,128,128]{4,3,2,1,0:T(8,128)S(1)} %exchange.1.gathered, s32[8,128]{1,0:T(8,128)S(1)} %get-tuple-element.7.rank_ref), custom_call_target="tpu_custom_call" | custom-call | tf_op jit(solution)/shard_map/finish/pallas_call | solution.py:636

commit v4 on v3

--- a/solution.py
+++ b/solution.py
@@ -39,8 +39,8 @@
 
 def prepare(
     dims, kern_hbm, thermal_hbm, kinetic_hbm, slot_hbm, tile_hbm, owner_hbm,
-    out_ref, ids_ref, rank_ref, kern_ref, slot_smem, thermal_ref, kinetic_ref, slot_ref, tile_ref, owner_ref,
-    thermal32, kinetic32, part_ref, split_ref, sems, small_sem,
+    split_ref, place_ref, ids_ref, rank_ref, kern_ref, slot_smem, thermal_ref, kinetic_ref, slot_ref,
+    tile_ref, owner_ref, thermal32, kinetic32, part_ref, sems, small_sem,
 ):
     vol_count, pix_count, slots, block_tiles, bucket = dims
     entries = kern_ref.shape[0]
@@ -101,7 +101,7 @@
     starts = dot(onehot(earlier), counts)
     inner = dot(onehot(earlier & same), counts)
     position = jnp.concatenate(position, axis=1)
-    place = (position + jnp.sum(ones * starts[:, 0:1], axis=0, keepdims=True)).astype(I32)
+    place_ref[...] = (position + jnp.sum(ones * starts[:, 0:1], axis=0, keepdims=True)).astype(I32)
     position = (position + jnp.sum(ones * inner[:, 0:1], axis=0, keepdims=True)).astype(I32)
 
     places = onehot(iota((bucket, slots), 0) == position)
@@ -152,7 +152,7 @@
             add_window(i, base_of(i))
             return unused
 
-        lax.fori_loop(q * per, (q + 1) * per, first_window, 0, unroll=4)
+        lax.fori_loop(q * per, (q + 1) * per, first_window, 0, unroll=16)
 
     def more_windows(i, unused):
         base = base_of(i)
@@ -164,33 +164,20 @@
 
         return lax.fori_loop(1, extra + 1, one, unused)
 
-    lax.fori_loop(0, blocks, more_windows, 0)
+    rows = slot_ref.shape[0] - lines + 1
+    ends = pltpu.roll(slot_ref[lines - 1:, :], 1, 1)
+    spans = ends - slot_ref[0:rows, :] // 8 * 8
+    first = (iota((rows, LANES), 1) == 0) & (iota((rows, LANES), 0) % lines == 0)
+
+    @pl.when(jnp.max(jnp.where(first, spans, 0)) >= WINDOW)
+    def _():
+        lax.fori_loop(0, blocks, more_windows, 0)
 
     split_ref[...] = halves(part_ref[0:slots, :])
 
-    cols, sub = LANES // half, bucket // half
-    lane = iota((sub, LANES), 1) // cols
-
-    def permute(q, unused):
-        moved = dot(onehot(iota((bucket, slots), 0) + q * bucket == place), split_ref[...])
-        for c in range(2):
-            high, low = c * LANES, (c + 2) * LANES
-            value = moved[:, high:high + LANES] + moved[:, low:low + LANES]
-            rolled = [value] + [pltpu.roll(value, d * cols, 1) for d in range(1, half)]
-            for h in range(half):
-                packed = rolled[(half - h) % half][0:sub]
-                for u in range(1, half):
-                    packed = jnp.where(
-                        lane == u, rolled[(u - h) % half][u * sub:(u + 1) * sub], packed
-                    )
-                out_ref[h, c, q] = packed
-        return unused
-
-    lax.fori_loop(0, half, permute, 0)
-
 
 def exchange(
-    dims, out_hbm, ids_hbm, gathered, arrived, ids, starts, rows_ref, acc, partial, swapped, sums,
+    dims, split_ref, place_ref, ids_hbm, gathered, out_ref, arrived, ids, starts, rows_ref, acc, partial, swapped, sums,
     crossed, total, send_sem, recv_sem, ids_send, ids_recv, local_sem, start_sem, swap_send,
     swap_recv, mid_send, mid_recv, far_send, far_recv, own_sem, pass_send, pass_recv,
 ):
@@ -237,6 +224,25 @@
     for k in range(1, pix_count):
         signal(vol, (pix + k) % pix_count)
     lax.fori_loop(chips, half * chips, greet, 0)
+
+    wide = iota((sub, LANES), 1) // cols
+    slots = place_ref.shape[1]
+
+    def permute(q):
+        moved = dot(onehot(iota((bucket, slots), 0) + q * bucket == place_ref[...]), split_ref[...])
+        for c in range(2):
+            high, low = c * LANES, (c + 2) * LANES
+            value = moved[:, high:high + LANES] + moved[:, low:low + LANES]
+            rolled = [value] + [pltpu.roll(value, d * cols, 1) for d in range(1, half)]
+            for h in range(half):
+                packed = rolled[(half - h) % half][0:sub]
+                for u in range(1, half):
+                    packed = jnp.where(
+                        wide == u, rolled[(u - h) % half][u * sub:(u + 1) * sub], packed
+                    )
+                out_ref[h, c, q] = packed
+
+    permute(0)
     pl.semaphore_wait(barrier, pix_count + (half - 1) * chips)
 
     def target(k):
@@ -246,7 +252,7 @@
     def rows_copy(q, k):
         other_place, other_channel = peer(k)
         return pltpu.make_async_remote_copy(
-            src_ref=out_hbm.at[other_place, other_channel, q], dst_ref=arrived.at[q, mine],
+            src_ref=out_ref.at[other_place, other_channel, q], dst_ref=arrived.at[q, mine],
             send_sem=send_sem.at[q, k], recv_sem=recv_sem.at[q, k],
             device_id=target(k), device_id_type=MESH,
         )
@@ -260,7 +266,7 @@
 
     def local_rows(q):
         return pltpu.make_async_copy(
-            out_hbm.at[place, channel, q], arrived.at[q, mine], local_sem.at[q]
+            out_ref.at[place, channel, q], arrived.at[q, mine], local_sem.at[q]
         )
 
     local_ids = pltpu.make_async_copy(ids_hbm, ids.at[mine], local_sem.at[half])
@@ -273,6 +279,10 @@
     local_ids.start()
 
     def send_chunk(q, unused):
+        @pl.when(q > 0)
+        def _():
+            permute(q)
+
         def one(k, unused):
             rows_copy(q, k).start()
             return unused
@@ -311,7 +321,6 @@
     lax.fori_loop(0, near_count, take_starts, 0)
 
     lane = iota((1, LANES), 1) // cols
-    wide = iota((sub, LANES), 1) // cols
     row = iota((bucket, LANES), 0)
     tile = iota((group_tiles, bucket), 0)
 
@@ -569,15 +578,16 @@
     half = vol_count // 2
     sub = bucket // half
     id_rows = vol_count * bucket // LANES + 8
-    outgoing, ids, rank = pl.pallas_call(
+    split, place, ids, rank = pl.pallas_call(
         functools.partial(prepare, (vol_count, pix_count, slots, block_tiles, bucket)),
         out_shape=(
-            jax.ShapeDtypeStruct((half, 2, half, sub, LANES), F32),
+            jax.ShapeDtypeStruct((slots, 2 * width), BF16),
+            jax.ShapeDtypeStruct((1, slots), I32),
             jax.ShapeDtypeStruct((id_rows, LANES), I32),
             jax.ShapeDtypeStruct((block_tiles // LANES, LANES), I32),
         ),
         in_specs=[hbm] * 6,
-        out_specs=(vmem, vmem, vmem),
+        out_specs=(vmem, vmem, vmem, vmem),
         scratch_shapes=[
             pltpu.VMEM(kernel.shape, BF16),
             pltpu.SMEM(shape, I32),
@@ -589,7 +599,6 @@
             pltpu.VMEM(shape, F32),
             pltpu.VMEM(shape, F32),
             pltpu.VMEM((slots + WINDOW, width), F32),
-            pltpu.VMEM((slots, 2 * width), BF16),
             dma((4,)),
             dma((6,)),
         ],
@@ -609,9 +618,10 @@
     gathered = pl.pallas_call(
         functools.partial(exchange, (vol_count, pix_count, block_tiles, bucket)),
         out_shape=jax.ShapeDtypeStruct((2, half, chips, share, LANES), F32),
-        in_specs=[anywhere, anywhere],
+        in_specs=[vmem, vmem, anywhere],
         out_specs=vmem,
         scratch_shapes=[
+            pltpu.VMEM((half, 2, half, sub, LANES), F32),
             pltpu.VMEM((half, near, sub, LANES), F32),
             pltpu.VMEM((near, id_rows, LANES), I32),
             pltpu.SMEM((near, LANES), I32),
@@ -631,7 +641,7 @@
             collective_id=0, has_side_effects=True, vmem_limit_bytes=EXCHANGE_VMEM
         ),
         name="exchange",
-    )(outgoing, ids)
+    )(split, place, ids)
 
     return pl.pallas_call(
         finish,

time: 49.8 us -> 43.3 us (0.87)
  Pallas kernels: 48.9 us -> 42.4 us
    pallas_call x1, Pallas kernels: 10.4 us -> 3.89 us  [shards(): pl.pallas_call(functools.partial(prepare, (vol_count, pix_count, slots, b...]
where the time goes in v4:
time: 43.3 us; the launch traced here: 43.1 us
  Pallas kernels  42.4 us (98%)
  between operations  0.65 us (2%)
    pallas_call x1, Pallas kernels, shards(): pl.pallas_call(functools.partial(exchange, (vol_count, pix_count, block_t...  36.2 us
    pallas_call x1, Pallas kernels, shards(): pl.pallas_call(functools.partial(prepare, (vol_count, pix_count, slots, b...  3.89 us
    pallas_call x1, Pallas kernels, shards(): pl.pallas_call(finish, out_shape=(jax.ShapeDtypeStruct((owned_most, width...  2.36 us

profile of v4, /device:TPU:29, one launch (start us, length us, event | category | flops | bytes accessed | tf_op | source)
XLA Modules:
  0.0 43.1 jit_solution(4810478305340826440)
XLA Ops:
  0.6 3.9 %prepare.1 = (bf16[1024,512]{1,0:T(8,128)(2,1)S(1)}, s32[1,1024]{1,0:T(1,128)S(1)}, s32[24,128]{1,0:T(8,128)S(1)}, s32[8,128]{1,0:T(8,128)S(1)}) custom-call(bf16[16384,128]{1,0:T(8,128)(2,1)} %kern_hbm.1, bf16[128,128]{1,0:T(8,128)(2,1)} %bitcast.5, bf16[128,128]{1,0:T(8,128)(2,1)} %bitcast.6, s32[128,128]{1,0:T(8,128)} %bitcast.4, s32[1,1024]{1,0:T(1,128)} %tile_hbm.1, ...), custom_call_target="tpu_custom_call" | custom-call | tf_op jit(solution)/shard_map/prepare/pallas_call | solution.py:581
  4.5 36.2 %exchange.1.gathered = f32[2,4,2,128,128]{4,3,2,1,0:T(8,128)S(1)} custom-call(bf16[1024,512]{1,0:T(8,128)(2,1)S(1)} %get-tuple-element.6.split_ref, s32[1,1024]{1,0:T(1,128)S(1)} %get-tuple-element.7.place_ref, s32[24,128]{1,0:T(8,128)S(1)} %get-tuple-element.8.ids_hbm), custom_call_target="tpu_custom_call" | custom-call | tf_op jit(solution)/shard_map/exchange/pallas_call | solution.py:618
  40.7 2.4 %finish.1 = (f32[512,256]{1,0:T(8,128)}, f32[1024,256]{1,0:T(8,128)}) custom-call(f32[2,4,2,128,128]{4,3,2,1,0:T(8,128)S(1)} %exchange.1.gathered, s32[8,128]{1,0:T(8,128)S(1)} %get-tuple-element.9.rank_ref), custom_call_target="tpu_custom_call" | custom-call | tf_op jit(solution)/shard_map/finish/pallas_call | solution.py:646

commit v5 on v4

--- a/solution.py
+++ b/solution.py
@@ -35,6 +35,20 @@
     high = x.astype(BF16)
     low = (x - high.astype(F32)).astype(BF16)
     return jnp.concatenate([high, low], axis=1)
+
+
+def turn_groups(values, lane, cols):
+    values = list(values)
+    step = 1
+    while step < len(values):
+        upper = lane // step % 2 == 1
+        for i in range(len(values)):
+            if i // step % 2 == 0:
+                a, b = values[i], values[i + step]
+                values[i] = jnp.where(upper, pltpu.roll(b, step * cols, 1), a)
+                values[i + step] = jnp.where(upper, b, pltpu.roll(a, LANES - step * cols, 1))
+        step *= 2
+    return values
 
 
 def prepare(
@@ -233,13 +247,8 @@
         for c in range(2):
             high, low = c * LANES, (c + 2) * LANES
             value = moved[:, high:high + LANES] + moved[:, low:low + LANES]
-            rolled = [value] + [pltpu.roll(value, d * cols, 1) for d in range(1, half)]
-            for h in range(half):
-                packed = rolled[(half - h) % half][0:sub]
-                for u in range(1, half):
-                    packed = jnp.where(
-                        wide == u, rolled[(u - h) % half][u * sub:(u + 1) * sub], packed
-                    )
+            parts = [value[u * sub:(u + 1) * sub] for u in range(half)]
+            for h, packed in enumerate(turn_groups(parts, wide, cols)):
                 out_ref[h, c, q] = packed
 
     permute(0)
@@ -372,10 +381,16 @@
             value = value + swapped[b, k - 1]
         return value
 
-    def mid_copy(b):
+    pieces = mid_send.shape[1]
+    piece_rows = share // pieces
+
+    def part(p):
+        return pl.ds(p * piece_rows, piece_rows)
+
+    def mid_copy(b, p):
         return pltpu.make_async_remote_copy(
-            src_ref=sums.at[b], dst_ref=crossed.at[b],
-            send_sem=mid_send.at[b], recv_sem=mid_recv.at[b],
+            src_ref=sums.at[b, part(p)], dst_ref=crossed.at[b, part(p)],
+            send_sem=mid_send.at[b, p], recv_sem=mid_recv.at[b, p],
             device_id=(across, pix), device_id_type=MESH,
         )
 
@@ -401,7 +416,8 @@
         lax.fori_loop(0, half, one, 0)
         swap(q)
         sums[q] = reduced(q)
-        mid_copy(q).start()
+        for p in range(pieces):
+            mid_copy(q, p).start()
         return unused
 
     lax.fori_loop(0, half, far, 0)
@@ -409,10 +425,10 @@
     def off(i):
         return (i + half - place) % half
 
-    def far_copy(i, k):
+    def far_copy(i, k, p):
         return pltpu.make_async_remote_copy(
-            src_ref=total.at[i], dst_ref=gathered.at[core, place, chip],
-            send_sem=far_send.at[off(i), k], recv_sem=far_recv.at[off(i), k],
+            src_ref=total.at[i, part(p)], dst_ref=gathered.at[core, place, chip, part(p)],
+            send_sem=far_send.at[off(i), k, p], recv_sem=far_recv.at[off(i), k, p],
             device_id=(side * half + i, (chip + k) % chips * 2 + core), device_id_type=MESH,
         )
 
@@ -421,20 +437,22 @@
 
     def finalize(i):
         value = reduced(half + i)
-        mid_copy(i).wait_recv()
-        total[i] = value + crossed[i]
-
-        @pl.when(i != place)
-        def _():
-            far_copy(i, 0).start()
+        for p in range(pieces):
+            mid_copy(i, p).wait_recv()
+            rows = slice(p * piece_rows, (p + 1) * piece_rows)
+            total[i, rows, :] = value[rows] + crossed[i, rows, :]
+
+            @pl.when(i != place)
+            def _():
+                far_copy(i, 0, p).start()
+
+            for k in range(1, chips):
+                far_copy(i, k, p).start()
 
         @pl.when(i == place)
         def _():
             own_copy().start()
 
-        for k in range(1, chips):
-            far_copy(i, k).start()
-
     def near(i, unused):
         acc[...] = jnp.zeros(acc.shape, F32)
 
@@ -454,51 +472,59 @@
     lax.fori_loop(0, half, near, 0)
     finalize(half - 1)
 
-    def pass_copy(o, k):
-        piece = gathered.at[core, (place + half - o) % half, (chip + chips - k) % chips]
+    def pass_copy(o, k, p):
+        piece = gathered.at[
+            core, (place + half - o) % half, (chip + chips - k) % chips, part(p)
+        ]
         return pltpu.make_async_remote_copy(
             src_ref=piece, dst_ref=piece,
-            send_sem=pass_send.at[o, k], recv_sem=pass_recv.at[o, k],
+            send_sem=pass_send.at[o, k, p], recv_sem=pass_recv.at[o, k, p],
             device_id=sibling, device_id_type=MESH,
         )
 
-    def far_arrival(o, k):
+    def far_arrival(o, k, p):
         return pltpu.make_async_remote_copy(
-            src_ref=total.at[0], dst_ref=gathered.at[core, place, chip],
-            send_sem=far_send.at[o, k], recv_sem=far_recv.at[o, k],
+            src_ref=total.at[0, part(p)], dst_ref=gathered.at[core, place, chip, part(p)],
+            send_sem=far_send.at[o, k, p], recv_sem=far_recv.at[o, k, p],
             device_id=(side * half + (place + o) % half, (chip + k) % chips * 2 + core),
             device_id_type=MESH,
         )
 
     own_copy().wait()
-    pass_copy(0, 0).start()
-    for k in range(1, chips):
-        far_arrival(0, k).wait_recv()
-        pass_copy(0, k).start()
-
-    def relay(o, unused):
-        for k in range(chips):
-            far_arrival(o, k).wait_recv()
-            pass_copy(o, k).start()
-        return unused
-
-    lax.fori_loop(1, half, relay, 0)
+    for p in range(pieces):
+        pass_copy(0, 0, p).start()
+    for p in range(pieces):
+        for k in range(1, chips):
+            far_arrival(0, k, p).wait_recv()
+            pass_copy(0, k, p).start()
+
+        def relay(o, unused):
+            for k in range(chips):
+                far_arrival(o, k, p).wait_recv()
+                pass_copy(o, k, p).start()
+            return unused
+
+        lax.fori_loop(1, half, relay, 0)
 
     def passed(o, unused):
         for k in range(chips):
-            pass_copy(o, k).wait()
+            for p in range(pieces):
+                pass_copy(o, k, p).wait()
         return unused
 
     lax.fori_loop(0, half, passed, 0)
-    for k in range(1, chips):
-        far_arrival(0, k).wait_send()
 
     def sent(o, unused):
-        for k in range(chips):
-            far_arrival(o, k).wait_send()
-        return unused
-
-    lax.fori_loop(1, half, sent, 0)
+        for p in range(pieces):
+            @pl.when(o > 0)
+            def _():
+                far_arrival(o, 0, p).wait_send()
+
+            for k in range(1, chips):
+                far_arrival(o, k, p).wait_send()
+        return unused
+
+    lax.fori_loop(0, half, sent, 0)
 
     def sent_rows(k, unused):
         ids_copy(k).wait_send()
@@ -513,7 +539,8 @@
     lax.fori_loop(1, near_count, sent_rows, 0)
 
     def sent_sums(b, unused):
-        mid_copy(b).wait_send()
+        for p in range(pieces):
+            mid_copy(b, p).wait_send()
         for k in range(1, members):
             swap_copy(b, k).wait_send()
             swap_copy(half + b, k).wait_send()
@@ -534,14 +561,9 @@
     for core in range(2):
         for chip in range(chips):
             first, channel = (chip // 2 * 2 + core) * share, chip % 2
-            rolled = []
-            for s in range(half):
-                value = gathered[core, s, chip]
-                rolled.append([value] + [pltpu.roll(value, d * cols, 1) for d in range(1, half)])
+            values = turn_groups([gathered[core, s, chip] for s in range(half)], lane, cols)
             for u in range(half):
-                value = rolled[0][(half - u) % half]
-                for s in range(1, half):
-                    value = jnp.where(lane == s, rolled[s][(s - u) % half], value)
+                value = values[u]
                 start = u * group_tiles + first
                 shell_ref[start:start + share, channel * LANES:(channel + 1) * LANES] = value
                 both = halves(value)
@@ -612,7 +634,7 @@
     ])
 
     chips = pix_count // 2
-    near = vol_count
+    near, pieces = vol_count, 1
     group_tiles = block_tiles // half
     share = group_tiles // chips
     gathered = pl.pallas_call(
@@ -634,8 +656,8 @@
             pltpu.VMEM((half, share, LANES), F32),
             dma((half, near)), dma((half, near)), dma((near,)), dma((near,)),
             dma((half + 1,)), dma((near,)), dma((vol_count, chips)), dma((vol_count, chips)),
-            dma((half,)), dma((half,)), dma((half, chips)), dma((half, chips)), dma,
-            dma((half, chips)), dma((half, chips)),
+            dma((half, pieces)), dma((half, pieces)), dma((half, chips, pieces)),
+            dma((half, chips, pieces)), dma, dma((half, chips, pieces)), dma((half, chips, pieces)),
         ],
         compiler_params=pltpu.CompilerParams(
             collective_id=0, has_side_effects=True, vmem_limit_bytes=EXCHANGE_VMEM

time: 43.3 us -> 42.9 us (level)
  no operation moved by 1% of the time
where the time goes in v5:
time: 42.9 us; the launch traced here: 42.7 us
  Pallas kernels  42.1 us (98%)
  between operations  0.65 us (2%)
    pallas_call x1, Pallas kernels, shards(): pl.pallas_call(functools.partial(exchange, (vol_count, pix_count, block_t...  36.2 us
    pallas_call x1, Pallas kernels, shards(): pl.pallas_call(functools.partial(prepare, (vol_count, pix_count, slots, b...  3.89 us
    pallas_call x1, Pallas kernels, shards(): pl.pallas_call(finish, out_shape=(jax.ShapeDtypeStruct((owned_most, width...  1.98 us

profile of v5, /device:TPU:29, one launch (start us, length us, event | category | flops | bytes accessed | tf_op | source)
XLA Modules:
  0.0 42.7 jit_solution(13780402463465911188)
XLA Ops:
  0.6 3.9 %prepare.1 = (bf16[1024,512]{1,0:T(8,128)(2,1)S(1)}, s32[1,1024]{1,0:T(1,128)S(1)}, s32[24,128]{1,0:T(8,128)S(1)}, s32[8,128]{1,0:T(8,128)S(1)}) custom-call(bf16[16384,128]{1,0:T(8,128)(2,1)} %kern_hbm.1, bf16[128,128]{1,0:T(8,128)(2,1)} %bitcast.5, bf16[128,128]{1,0:T(8,128)(2,1)} %bitcast.6, s32[128,128]{1,0:T(8,128)} %bitcast.4, s32[1,1024]{1,0:T(1,128)} %tile_hbm.1, ...), custom_call_target="tpu_custom_call" | custom-call | tf_op jit(solution)/shard_map/prepare/pallas_call | solution.py:603
  4.5 36.2 %exchange.1.gathered = f32[2,4,2,128,128]{4,3,2,1,0:T(8,128)S(1)} custom-call(bf16[1024,512]{1,0:T(8,128)(2,1)S(1)} %get-tuple-element.6.split_ref, s32[1,1024]{1,0:T(1,128)S(1)} %get-tuple-element.7.place_ref, s32[24,128]{1,0:T(8,128)S(1)} %get-tuple-element.8.ids_hbm), custom_call_target="tpu_custom_call" | custom-call | tf_op jit(solution)/shard_map/exchange/pallas_call | solution.py:640
  40.8 2.0 %finish.1 = (f32[512,256]{1,0:T(8,128)}, f32[1024,256]{1,0:T(8,128)}) custom-call(f32[2,4,2,128,128]{4,3,2,1,0:T(8,128)S(1)} %exchange.1.gathered, s32[8,128]{1,0:T(8,128)S(1)} %get-tuple-element.9.rank_ref), custom_call_target="tpu_custom_call" | custom-call | tf_op jit(solution)/shard_map/finish/pallas_call | solution.py:668

commit v6 on v5

--- a/solution.py
+++ b/solution.py
@@ -10,7 +10,7 @@
 MESH = pl.DeviceIdType.MESH
 LANES = 128
 BLOCK = 256
-WINDOW = 48
+WINDOW = 40
 F32 = jnp.float32
 BF16 = jnp.bfloat16
 I32 = jnp.int32
@@ -166,7 +166,7 @@
             add_window(i, base_of(i))
             return unused
 
-        lax.fori_loop(q * per, (q + 1) * per, first_window, 0, unroll=16)
+        lax.fori_loop(q * per, (q + 1) * per, first_window, 0, unroll=32)
 
     def more_windows(i, unused):
         base = base_of(i)
@@ -394,7 +394,7 @@
             device_id=(across, pix), device_id_type=MESH,
         )
 
-    def far(q, unused):
+    def far_sum(q):
         acc[...] = jnp.zeros(acc.shape, F32)
 
         def one(p, unused):
@@ -415,9 +415,30 @@
 
         lax.fori_loop(0, half, one, 0)
         swap(q)
+
+    def near_sum(i, unused):
+        acc[...] = jnp.zeros(acc.shape, F32)
+
+        def some(p, unused):
+            accumulate(half + i, [4 * p + j for j in range(4)])
+            return unused
+
+        lax.fori_loop(0, near_count // 4, some, 0)
+        swap(half + i)
+        return unused
+
+    def send_far(q):
         sums[q] = reduced(q)
         for p in range(pieces):
             mid_copy(q, p).start()
+
+    def far(q, unused):
+        far_sum(q)
+
+        @pl.when(q > 0)
+        def _():
+            send_far(q - 1)
+
         return unused
 
     lax.fori_loop(0, half, far, 0)
@@ -453,24 +474,22 @@
         def _():
             own_copy().start()
 
-    def near(i, unused):
-        acc[...] = jnp.zeros(acc.shape, F32)
-
-        def some(p, unused):
-            accumulate(half + i, [4 * p + j for j in range(4)])
-            return unused
-
-        lax.fori_loop(0, near_count // 4, some, 0)
-        swap(half + i)
-
-        @pl.when(i > 0)
-        def _():
-            finalize(i - 1)
-
-        return unused
-
-    lax.fori_loop(0, half, near, 0)
-    finalize(half - 1)
+    early = 2
+    lax.fori_loop(0, early, near_sum, 0)
+    send_far(half - 1)
+
+    def finish_near(i, unused):
+        near_sum(i, 0)
+        finalize(i - 1)
+        return unused
+
+    def finish_last(i, unused):
+        finalize(i)
+        return unused
+
+    finalize(0)
+    lax.fori_loop(early, half, finish_near, 0)
+    lax.fori_loop(half - 1, half, finish_last, 0)
 
     def pass_copy(o, k, p):
         piece = gathered.at[
@@ -621,7 +640,7 @@
             pltpu.VMEM(shape, F32),
             pltpu.VMEM(shape, F32),
             pltpu.VMEM((slots + WINDOW, width), F32),
-            dma((4,)),
+            dma((2,)),
             dma((6,)),
         ],
         compiler_params=pltpu.CompilerParams(vmem_limit_bytes=PREPARE_VMEM),

time: 42.9 us -> 42.8 us (level)
  no operation moved by 1% of the time
where the time goes in v6:
time: 42.8 us; the launch traced here: 42.4 us
  Pallas kernels  41.7 us (97%)
  between operations  0.65 us (2%)
    pallas_call x1, Pallas kernels, shards(): pl.pallas_call(functools.partial(exchange, (vol_count, pix_count, block_t...  36.1 us
    pallas_call x1, Pallas kernels, shards(): pl.pallas_call(functools.partial(prepare, (vol_count, pix_count, slots, b...  3.61 us
    pallas_call x1, Pallas kernels, shards(): pl.pallas_call(finish, out_shape=(jax.ShapeDtypeStruct((owned_most, width...  1.98 us

profile of v6, /device:TPU:29, one launch (start us, length us, event | category | flops | bytes accessed | tf_op | source)
XLA Modules:
  0.0 42.4 jit_solution(17839531055396868676)
XLA Ops:
  0.6 3.6 %prepare.1 = (bf16[1024,512]{1,0:T(8,128)(2,1)S(1)}, s32[1,1024]{1,0:T(1,128)S(1)}, s32[24,128]{1,0:T(8,128)S(1)}, s32[8,128]{1,0:T(8,128)S(1)}) custom-call(bf16[16384,128]{1,0:T(8,128)(2,1)} %kern_hbm.1, bf16[128,128]{1,0:T(8,128)(2,1)} %bitcast.5, bf16[128,128]{1,0:T(8,128)(2,1)} %bitcast.6, s32[128,128]{1,0:T(8,128)} %bitcast.4, s32[1,1024]{1,0:T(1,128)} %tile_hbm.1, ...), custom_call_target="tpu_custom_call" | custom-call | tf_op jit(solution)/shard_map/prepare/pallas_call | solution.py:622
  4.2 36.1 %exchange.1.gathered = f32[2,4,2,128,128]{4,3,2,1,0:T(8,128)S(1)} custom-call(bf16[1024,512]{1,0:T(8,128)(2,1)S(1)} %get-tuple-element.6.split_ref, s32[1,1024]{1,0:T(1,128)S(1)} %get-tuple-element.7.place_ref, s32[24,128]{1,0:T(8,128)S(1)} %get-tuple-element.8.ids_hbm), custom_call_target="tpu_custom_call" | custom-call | tf_op jit(solution)/shard_map/exchange/pallas_call | solution.py:659
  40.4 2.0 %finish.1 = (f32[512,256]{1,0:T(8,128)}, f32[1024,256]{1,0:T(8,128)}) custom-call(f32[2,4,2,128,128]{4,3,2,1,0:T(8,128)S(1)} %exchange.1.gathered, s32[8,128]{1,0:T(8,128)S(1)} %get-tuple-element.9.rank_ref), custom_call_target="tpu_custom_call" | custom-call | tf_op jit(solution)/shard_map/finish/pallas_call | solution.py:687
